TPU v7x, 256 devices: a whole 4x4x8 slice. The times are simulated.
256 devices in a mesh: seq: 32 (over z, x), head: 8 (over y, core).
Axes of the slice: x: 4, y: 4, z: 8, core: 2. Of those that a mesh axis runs over, the one named last changes fastest.
Arguments:
- queries: bfloat16 [16384, 1024], P('seq', 'head'), may hold values from -6 to 6
- keys: bfloat16 [16384, 1024], P('seq', 'head'), may hold values from -5 to 5
- values: bfloat16 [16384, 1024], P('seq', 'head'), may hold values from -6 to 6
- ridge: float32 [8], P('head'), may hold values from 0.5 to 4
- gain: float32 [1024], P('head'), may hold values from 0.5 to 1.5
- grad_out: bfloat16 [16384, 1024], P('seq', 'head'), may hold values from -6 to 6
Outputs:
- output: bfloat16 [16384, 1024], P('seq', 'head')
- grad_queries: bfloat16 [16384, 1024], P('seq', 'head')
- grad_keys: bfloat16 [16384, 1024], P('seq', 'head')
- grad_values: bfloat16 [16384, 1024], P('seq', 'head')
- grad_gain: float32 [1024], P('head')
All inputs are finite; a program needn't handle non-finite values.
Results may differ from a plain program's by a relative error of at most 0.0044.
Values sent between devices are 32-bit elements; how exact they have to be, the bound alone decides.
No kernel may reach another device: no remote copies, remote signals or barrier semaphores. Data moves between devices by JAX's collectives and lax.ppermute only.
A program may use at most 64 MiB of HBM per device.

v0:
```python
import jax
import jax.numpy as jnp
from jax import lax
from jax.sharding import Mesh
from jax.sharding import PartitionSpec as P

HEADS = 8
D = 128
CG_STEPS = 6
SEQ = ("seq_0", "seq_1")


EPS = 1e-06
HIGH = lax.Precision.HIGHEST
BLOCK_ROWS = 256


def neutral_like(x, identity):
    return jax.tree.map(
        lambda a, e: jnp.broadcast_to(jnp.asarray(e, a.dtype), a.shape), x, identity
    )


def prefix_by_axis(x, axes, combine, identity, reverse):
    before = start = neutral_like(x, identity)
    running = x
    for axis in reversed(axes):
        size, index = (lax.axis_size(axis), lax.axis_index(axis))
        pieces = jax.tree.map(lambda part: lax.all_gather(part, axis), running)
        inside, running = (start, start)
        for k in reversed(range(size)) if reverse else range(size):
            passed = k > index if reverse else k < index
            running = combine(running, jax.tree.map(lambda part: part[k], pieces))
            inside = jax.tree.map(lambda new, old: jnp.where(passed, new, old), running, inside)
        before = combine(inside, before)
    return before


def sent_to_all(x, axis):
    copies = jnp.broadcast_to(x, (lax.axis_size(axis), *x.shape))
    return lax.all_to_all(copies, axis, split_axis=0, concat_axis=0, tiled=True)


def of_everyone(x, axis):
    return sent_to_all(x, axis).sum(axis=0)


def matmul(left, right):
    return jnp.dot(left, right, precision=HIGH)


def rows_by_rows(left, right):
    return lax.dot_general(left, right, (((1,), (1,)), ((), ())), precision=HIGH)


def cols_by_cols(left, right):
    return lax.dot_general(left, right, (((0,), (0,)), ((), ())), precision=HIGH)


def lower_mask(count):
    rows = lax.broadcasted_iota(jnp.int32, (count, count), 0)
    cols = lax.broadcasted_iota(jnp.int32, (count, count), 1)
    return (rows >= cols).astype(jnp.float32)


def conjugate(apply_fn, rhs):
    solution = jnp.zeros_like(rhs)
    resid = rhs
    search = rhs
    norm_now = jnp.sum(resid * resid, axis=-1, keepdims=True)
    for _ in range(CG_STEPS):
        image = apply_fn(search)
        alpha = norm_now / (jnp.sum(search * image, axis=-1, keepdims=True) + EPS)
        solution = solution + alpha * search
        resid = resid - alpha * image
        norm_next = jnp.sum(resid * resid, axis=-1, keepdims=True)
        search = resid + norm_next / (norm_now + EPS) * search
        norm_now = norm_next
    return solution


def make_apply(gram_prev, keys_blk, ridge, mask):

    def apply_fn(search):
        return (
            matmul(search, gram_prev)
            + matmul(mask * rows_by_rows(search, keys_blk), keys_blk)
            + ridge * search
        )

    return apply_fn


def forward_block(queries_blk, keys_blk, values_blk, gram_prev, assoc_prev, ridge):
    mask = lower_mask(queries_blk.shape[0])
    solved = conjugate(make_apply(gram_prev, keys_blk, ridge, mask), queries_blk)
    mixed = rows_by_rows(solved, assoc_prev) + matmul(
        mask * rows_by_rows(solved, keys_blk), values_blk
    )
    return (solved, mixed)


def adjoint_block(keys_blk, values_blk, gram_prev, assoc_prev, ridge, solved, grad_mixed):
    mask = lower_mask(keys_blk.shape[0])
    rhs = matmul(grad_mixed, assoc_prev) + matmul(
        mask * rows_by_rows(grad_mixed, values_blk), keys_blk
    )
    adjoint = conjugate(make_apply(gram_prev, keys_blk, ridge, mask), rhs)
    suffix_loc = cols_by_cols(grad_mixed, solved)
    pair = cols_by_cols(adjoint, solved)
    return (adjoint, suffix_loc, pair + pair.T)


def grads_block(keys_blk, values_blk, solved, adjoint, grad_mixed, suffix_next, pairs_next):
    upper = lower_mask(keys_blk.shape[0]).T
    key_solved = upper * rows_by_rows(keys_blk, solved)
    grad_values = rows_by_rows(keys_blk, suffix_next) + matmul(key_solved, grad_mixed)
    grad_keys = (
        matmul(values_blk, suffix_next)
        + matmul(upper * rows_by_rows(values_blk, grad_mixed), solved)
        - matmul(keys_blk, pairs_next)
        - matmul(key_solved, adjoint)
        - matmul(upper * rows_by_rows(keys_blk, adjoint), solved)
    )
    return (grad_keys, grad_values)


def add_pair(earlier, later):
    return (earlier[0] + later[0], earlier[1] + later[1])


def head_grams(left, right):
    return jax.vmap(cols_by_cols, in_axes=(1, 1))(left, right)


def per_device(queries, keys, values, ridge, gain, grad_out):
    tok = queries.shape[0]
    heads_here = ridge.shape[0]
    rows_blk = BLOCK_ROWS
    blocks = tok // rows_blk

    def split(array):
        return array.astype(jnp.float32).reshape(blocks, rows_blk, heads_here, D)

    def merge_rows(array):
        return array.reshape(tok, heads_here * D)

    query_f = split(queries)
    key_f = split(keys)
    value_f = split(values)
    zeros = jnp.zeros((heads_here, D, D), jnp.float32)
    gram_blk = jax.vmap(head_grams)(key_f, key_f)
    assoc_blk = jax.vmap(head_grams)(value_f, key_f)
    gram_run = jnp.cumsum(gram_blk, axis=0)
    assoc_run = jnp.cumsum(assoc_blk, axis=0)
    gram_loc = gram_run[-1]
    assoc_loc = assoc_run[-1]
    gram_prev, assoc_prev = prefix_by_axis(
        (gram_loc, assoc_loc), SEQ, add_pair, (zeros, zeros), False
    )
    gram_each = gram_prev[None] + (gram_run - gram_blk)
    assoc_each = assoc_prev[None] + (assoc_run - assoc_blk)
    heads_fwd = jax.vmap(forward_block, in_axes=(1, 1, 1, 0, 0, 0), out_axes=1)
    solved, mixed = jax.vmap(heads_fwd, in_axes=(0, 0, 0, 0, 0, None))(
        query_f, key_f, value_f, gram_each, assoc_each, ridge
    )
    squares = lax.psum(jnp.sum(mixed * mixed, axis=(2, 3)), "head")
    denom = jnp.sqrt(squares / (HEADS * D) + EPS)[:, :, None, None]
    gains = gain.reshape(1, 1, heads_here, D)
    output = merge_rows((mixed * gains / denom).astype(jnp.bfloat16))
    upstream = split(grad_out)
    gain_part = jnp.sum(upstream * mixed / denom, axis=(0, 1))
    centre = lax.psum(jnp.sum(gains * upstream * mixed, axis=(2, 3)), "head")[:, :, None, None]
    grad_mixed = gains * upstream / denom - mixed * centre / (denom**3 * (HEADS * D))
    heads_adj = jax.vmap(adjoint_block, in_axes=(1, 1, 0, 0, 0, 1, 1), out_axes=(1, 0, 0))
    adjoint, suffix_blk, pairs_blk = jax.vmap(heads_adj, in_axes=(0, 0, 0, 0, None, 0, 0))(
        key_f, value_f, gram_each, assoc_each, ridge, solved, grad_mixed
    )
    suffix_run = jnp.cumsum(suffix_blk, axis=0)
    pairs_run = jnp.cumsum(pairs_blk, axis=0)
    suffix_loc = suffix_run[-1]
    pairs_loc = pairs_run[-1]
    suffix_next, pairs_next = prefix_by_axis(
        (suffix_loc, pairs_loc), SEQ, add_pair, (zeros, zeros), True
    )
    suffix_each = suffix_next[None] + (suffix_loc[None] - suffix_run)
    pairs_each = pairs_next[None] + (pairs_loc[None] - pairs_run)
    heads_grad = jax.vmap(grads_block, in_axes=(1, 1, 1, 1, 1, 0, 0), out_axes=1)
    grad_keys, grad_values = jax.vmap(heads_grad)(
        key_f, value_f, solved, adjoint, grad_mixed, suffix_each, pairs_each
    )
    grad_gain = of_everyone(gain_part, SEQ).reshape(heads_here * D)
    return (
        output,
        merge_rows(adjoint.astype(jnp.bfloat16)),
        merge_rows(grad_keys.astype(jnp.bfloat16)),
        merge_rows(grad_values.astype(jnp.bfloat16)),
        grad_gain,
    )


def solution(mesh):
    split = Mesh(mesh.devices.reshape(8, 4, mesh.shape["head"]), ("seq_0", "seq_1", "head"))
    return jax.shard_map(
        per_device,
        mesh=split,
        in_specs=(
            P(SEQ, "head"),
            P(SEQ, "head"),
            P(SEQ, "head"),
            P("head"),
            P("head"),
            P(SEQ, "head"),
        ),
        out_specs=(P(SEQ, "head"), P(SEQ, "head"), P(SEQ, "head"), P(SEQ, "head"), P("head")),
        check_vma=False,
    )
```

profile of v0, /device:TPU:8, one launch (start us, length us, event | category | flops | bytes accessed | tf_op | source)
XLA Modules:
  0.0 208.1 jit_solution(16235690133060428820)
XLA Ops:
  2.1 12.6 %all_gather.28 = f32[4,1,128,128]{3,2,1,0:T(8,128)S(1)} all-gather(f32[1,1,128,128]{3,2,1,0:T(8,128)S(1)} %slice_bitcast_fusion.1), channel_id=1, replica_groups=mesh['seq_0'=8,'seq_1'=4,'head'=8] {'seq_1'}, dimensions={0}, use_global_device_ids=true | all-gather | bytes 327680 | tf_op jit(solution)/shard_map/all_gather | solution.py:29
  14.9 28.9 %all_gather.29 = f32[8,1,128,128]{3,2,1,0:T(8,128)S(1)} all-gather(f32[1,1,128,128]{3,2,1,0:T(8,128)S(1)} %slice_add_fusion.37), channel_id=1, replica_groups=mesh['seq_0'=8,'seq_1'=4,'head'=8] {'seq_0'}, dimensions={0}, use_global_device_ids=true | all-gather | bytes 589824 | tf_op jit(solution)/shard_map/all_gather | solution.py:29
  44.5 0.5 multiply_reduce_fusion.22
  50.4 0.5 multiply_reduce_fusion.14
  52.7 12.3 %all_gather.30 = f32[4,1,128,128]{3,2,1,0:T(8,128)S(1)} all-gather(f32[1,1,128,128]{3,2,1,0:T(8,128)S(1)} %slice_bitcast_fusion), channel_id=1, replica_groups=mesh['seq_0'=8,'seq_1'=4,'head'=8] {'seq_1'}, dimensions={0}, use_global_device_ids=true | all-gather | bytes 327680 | tf_op jit(solution)/shard_map/all_gather | solution.py:29
  65.0 0.9 copy-done.3
  65.9 25.3 %all_gather.31 = f32[8,1,128,128]{3,2,1,0:T(8,128)S(1)} all-gather(f32[1,1,128,128]{3,2,1,0:T(8,128)S(1)} %slice_add_fusion.27), channel_id=1, replica_groups=mesh['seq_0'=8,'seq_1'=4,'head'=8] {'seq_0'}, dimensions={0}, use_global_device_ids=true | all-gather | bytes 589824 | tf_op jit(solution)/shard_map/all_gather | solution.py:29
  92.4 0.6 fusion.65
  93.0 0.6 copy-done.4
  93.6 0.6 multiply_reduce_fusion.11
  94.2 10.0 %all-reduce = (f32[2,256]{1,0:T(2,128)S(1)}, f32[2,256]{1,0:T(2,128)S(1)}) all-reduce(f32[2,256]{1,0:T(2,128)S(1)} %get-tuple-element.8, f32[2,256]{1,0:T(2,128)S(1)} %get-tuple-element.7), channel_id=1, replica_groups=mesh['seq_0'=8,'seq_1'=4,'head'=8] {'head'}, use_global_device_ids=true, to_apply=%region_15.16 | all-reduce | flops 1024 | bytes 8192 | tf_op jit(solution)/shard_map/psum | solution.py:167
  104.2 0.8 fusion.30
  105.0 0.6 broadcast_in_dim.5
  105.6 7.2 %all-to-all-start = ((f32[32,1,128]{2,1,0:T(1,128)}), f32[32,1,128]{2,1,0:T(1,128)S(1)}, u32[]{:S(2)}, u32[]{:S(2)}) async-start(f32[32,1,128]{2,1,0:T(1,128)} %broadcast_in_dim.5), calls=%async_computation | async-start | bytes 32768 | tf_op jit(solution)/shard_map/all_to_all | solution.py:41
  113.6 0.6 convolution_bitcast_fusion.6
  114.3 12.9 %all_gather.32 = f32[4,1,128,128]{3,2,1,0:T(8,128)S(1)} all-gather(f32[1,1,128,128]{3,2,1,0:T(8,128)S(1)} %get-tuple-element.29), channel_id=1, replica_groups=mesh['seq_0'=8,'seq_1'=4,'head'=8] {'seq_1'}, dimensions={0}, use_global_device_ids=true | all-gather | bytes 327680 | tf_op jit(solution)/shard_map/all_gather | solution.py:29
  127.2 26.4 %all_gather.33 = f32[8,1,128,128]{3,2,1,0:T(8,128)S(1)} all-gather(f32[1,1,128,128]{3,2,1,0:T(8,128)S(1)} %slice_add_fusion.17), channel_id=1, replica_groups=mesh['seq_0'=8,'seq_1'=4,'head'=8] {'seq_0'}, dimensions={0}, use_global_device_ids=true | all-gather | bytes 589824 | tf_op jit(solution)/shard_map/all_gather | solution.py:29
  164.9 0.7 fusion.17
  166.2 12.3 %all_gather.34 = f32[4,1,128,128]{3,2,1,0:T(8,128)S(1)} all-gather(f32[1,1,128,128]{3,2,1,0:T(8,128)S(1)} %get-tuple-element.27), channel_id=1, replica_groups=mesh['seq_0'=8,'seq_1'=4,'head'=8] {'seq_1'}, dimensions={0}, use_global_device_ids=true | all-gather | bytes 327680 | tf_op jit(solution)/shard_map/all_gather | solution.py:29
  178.4 25.5 %all_gather.35 = f32[8,1,128,128]{3,2,1,0:T(8,128)S(1)} all-gather(f32[1,1,128,128]{3,2,1,0:T(8,128)S(1)} %slice_add_fusion.7), channel_id=1, replica_groups=mesh['seq_0'=8,'seq_1'=4,'head'=8] {'seq_0'}, dimensions={0}, use_global_device_ids=true | all-gather | bytes 589824 | tf_op jit(solution)/shard_map/all_gather | solution.py:29
  205.3 0.8 copy.382
  206.0 0.8 copy.360
  206.8 0.8 copy.379
  207.6 0.5 reduce_sum.279
  (128 shorter events, 23.3 us)
Async XLA Ops:
  0.6 1.1 copy-start
  0.7 0.9 copy-start.2
  51.5 0.9 copy-start.1
  65.0 0.9 copy-start.3
  93.0 0.7 copy-start.4
  105.6 101.9 %all-to-all-start = ((f32[32,1,128]{2,1,0:T(1,128)}), f32[32,1,128]{2,1,0:T(1,128)S(1)}, u32[]{:S(2)}, u32[]{:S(2)}) async-start(f32[32,1,128]{2,1,0:T(1,128)} %broadcast_in_dim.5), calls=%async_computation | async-start | bytes 32768 | tf_op jit(solution)/shard_map/all_to_all | solution.py:41
where the time goes:
time: 210 us; the launch traced here: 208 us
  blocking collectives  166 us (79%)
  matrix products  23.3 us (11%)
  starting transfers between devices  7.18 us (3%)
  local copies, waits for them, and re-layouts  5.35 us (3%)
  other arithmetic  3.83 us (2%)
  between operations  2.21 us (1%)
    all_gather x8, blocking collectives, prefix_by_axis(): pieces = jax.tree.map(lambda part: lax.all_gather(part, axis), running)  156 us
    dot_general x33, matrix products, matmul(): return jnp.dot(left, right, precision=HIGH)  14.9 us
    psum x1, blocking collectives, per_device(): squares = lax.psum(jnp.sum(mixed * mixed, axis=(2, 3)), 'head')  10 us
    all_to_all x1, starting transfers between devices, sent_to_all(): return lax.all_to_all(copies, axis, split_axis=0, concat_axis=0, tiled=True)  7.18 us
    dot_general x17, matrix products, rows_by_rows(): lax.dot_general(left, right, (((1,), (1,)), ((), ())), precision=HIGH)  6.91 us
  transfers between devices with their start and end apart: 1, of which 0 were waited for; matrix products, arithmetic and copies ran while one was open for 8% of the time, Pallas kernels for 0%

commit v1 on v0

v1 whole, which is shorter than its diff:
```python
import jax
import jax.numpy as jnp
from jax import lax
from jax.experimental import pallas as pl
from jax.experimental.pallas import tpu as pltpu
from jax.sharding import Mesh
from jax.sharding import PartitionSpec as P

HEADS = 8
D = 128
CG_STEPS = 6
EPS = 1e-06
ZN = 8
XN = 4
SEQ = ("z", "x")
C = 128
F32 = jnp.float32
BF16 = jnp.bfloat16
VMEM = pl.BlockSpec(memory_space=pltpu.VMEM)
SMEM = pl.BlockSpec(memory_space=pltpu.SMEM)


def split2(x):
    high = x.astype(BF16)
    return high, (x - high.astype(F32)).astype(BF16)


def mm(left, right):
    return jnp.dot(left, right, preferred_element_type=F32)


def mm_t(left, right):
    return lax.dot_general(left, right, (((0,), (0,)), ((), ())), preferred_element_type=F32)


def lanes(*parts):
    return jnp.concatenate(parts, axis=1)


def rows(*parts):
    return jnp.concatenate(parts, axis=0)


def iota2(axis):
    return lax.broadcasted_iota(jnp.int32, (C, C), axis)


def row_sum(x):
    return jnp.sum(x, axis=-1, keepdims=True)


def call(kernel, outs, ins, args, flops, scratch=()):
    size = sum(a.size * a.dtype.itemsize for a in args)
    return pl.pallas_call(
        kernel,
        out_shape=[jax.ShapeDtypeStruct(s, t) for s, t in outs],
        in_specs=ins,
        out_specs=[VMEM] * len(outs),
        scratch_shapes=list(scratch),
        cost_estimate=pl.CostEstimate(flops=flops, bytes_accessed=size, transcendentals=0),
    )(*args)


def masked_apply(left, wide, tall, keep):
    high, low = split2(left)
    both = mm(lanes(high, low), wide)
    inner = jnp.where(keep, both[:, :C], 0.0)
    s_high, s_low = split2(inner)
    return both[:, C:] + mm(lanes(s_high, s_low, high), tall)


def conjugate(rhs, apply_fn):
    count = len(rhs)
    each = range(count)
    sol = [None] * count
    res = list(rhs)
    sea = list(rhs)
    now = [row_sum(r * r) for r in res]
    for step in range(CG_STEPS):
        image = [apply_fn(c, sea[c]) for c in each]
        alpha = [now[c] / (row_sum(sea[c] * image[c]) + EPS) for c in each]
        sol = [alpha[c] * sea[c] if step == 0 else sol[c] + alpha[c] * sea[c] for c in each]
        if step == CG_STEPS - 1:
            break
        res = [res[c] - alpha[c] * image[c] for c in each]
        new = [row_sum(res[c] * res[c]) for c in each]
        sea = [res[c] + new[c] / (now[c] + EPS) * sea[c] for c in each]
        now = new
    return sol


def gram_kernel(k_ref, v_ref, out_ref):
    k = k_ref[...]
    both = mm_t(lanes(k, v_ref[...]), k)
    for j in range(XN):
        out_ref[j, :32] = both[32 * j : 32 * j + 32]
        out_ref[j, 32:] = both[D + 32 * j : D + 32 * j + 32]


def total_kernel(a_ref, out_ref):
    total = a_ref[0] + a_ref[1] + a_ref[2] + a_ref[3]
    for z in range(ZN):
        out_ref[z] = total


def before_kernel(z_ref, a_ref, b_ref, out_ref):
    z = z_ref[0]
    run = jnp.where(z > 0, b_ref[0], 0.0)
    for k in range(1, ZN - 1):
        run = run + jnp.where(k < z, b_ref[k], 0.0)
    for j in range(XN):
        out_ref[j] = run
        if j < XN - 1:
            run = run + a_ref[j]


def after_kernel(z_ref, a_ref, b_ref, out_ref, gain_ref):
    z = z_ref[0]
    run = jnp.where(z < ZN - 1, b_ref[ZN - 1, :64], 0.0)
    for k in range(1, ZN - 1):
        run = run + jnp.where(k > z, b_ref[k, :64], 0.0)
    for j in reversed(range(XN)):
        out_ref[j] = run
        if j > 0:
            run = run + a_ref[j, :64]
    gain = b_ref[0, 64:]
    for k in range(1, ZN):
        gain = gain + b_ref[k, 64:]
    gain_ref[...] = gain


def quarters(ref, start):
    return rows(*[ref[j, start : start + 32] for j in range(XN)])


def forward_kernel(ridge_ref, q_ref, k_ref, v_ref, g_ref, gain_ref, state_ref,
                   solved_ref, mixed_ref, sums_ref, wide_ref, tall_ref, assoc_ref):
    chunks = q_ref.shape[0] // C
    each = range(chunks)
    at = [slice(C * c, C * c + C) for c in each]
    keep = iota2(0) >= iota2(1)
    eye = iota2(0) == iota2(1)
    gram = quarters(state_ref, 0) + jnp.where(eye, ridge_ref[0], 0.0)
    assoc = quarters(state_ref, 32)
    turned = []
    for c in each:
        k = k_ref[at[c]]
        v = v_ref[at[c]]
        k_t = k.T
        turned.append(k_t)
        high, low = split2(gram)
        top = lanes(k_t, high)
        wide_ref[c, :C] = top
        wide_ref[c, C:] = top
        tall_ref[c] = rows(k, k, low)
        assoc_ref[c] = assoc
        if c < chunks - 1:
            more = mm(rows(k_t, v.T), k)
            gram = gram + more[:C]
            assoc = assoc + more[C:]
    solved = conjugate(
        [q_ref[at[c]].astype(F32) for c in each],
        lambda c, p: masked_apply(p, wide_ref[c], tall_ref[c], keep),
    )
    gain = gain_ref[...]
    ones = jnp.ones((8, 2 * D), BF16)
    for c in each:
        high, low = split2(assoc_ref[c].T)
        top = lanes(turned[c], high)
        v = v_ref[at[c]]
        mixed = masked_apply(solved[c], rows(top, top), rows(v, v, low), keep)
        solved_ref[at[c]] = solved[c]
        mixed_ref[at[c]] = mixed
        square = mixed * mixed
        cross = gain * g_ref[at[c]].astype(F32) * mixed
        for n, x in enumerate((square, cross)):
            total = lax.dot_general(
                ones, lanes(*split2(x)), (((1,), (1,)), ((), ())), preferred_element_type=F32
            )
            row = 4 * n + c
            for h in range(HEADS):
                sums_ref[h, row : row + 1] = total[:1]


def adjoint_kernel(k_ref, v_ref, g_ref, gain_ref, sums_ref, solved_ref, mixed_ref, wide_ref, tall_ref, assoc_ref,
                   out_ref, grad_q_ref, adjoint_ref, grad_mixed_ref, part_ref):
    chunks = k_ref.shape[0] // C
    each = range(chunks)
    at = [slice(C * c, C * c + C) for c in each]
    keep = iota2(0) >= iota2(1)
    gain = gain_ref[...]
    sums = sums_ref[0]
    for h in range(1, HEADS):
        sums = sums + sums_ref[h]
    columns = rows(sums, jnp.zeros((C - 8, C), F32)).T
    rhs = []
    gain_part = jnp.zeros((1, D), F32)
    grads = []
    for c in each:
        denom = jnp.sqrt(columns[:, c : c + 1] / (HEADS * D) + EPS)
        inverse = 1.0 / denom
        factor = columns[:, 4 + c : 5 + c] / (denom * denom * denom * (HEADS * D))
        mixed = mixed_ref[at[c]]
        scaled = mixed * inverse
        upstream = g_ref[at[c]].astype(F32)
        out_ref[at[c]] = (scaled * gain).astype(BF16)
        gain_part = gain_part + jnp.sum(upstream * scaled, axis=0, keepdims=True)
        grad = gain * upstream * inverse - mixed * factor
        grads.append(grad)
        grad_mixed_ref[at[c]] = grad
        k = k_ref[at[c]]
        high, low = split2(assoc_ref[c])
        top = lanes(v_ref[at[c]].T, high)
        rhs.append(masked_apply(grad, rows(top, top), rows(k, k, low), keep))
    adjoint = conjugate(rhs, lambda c, p: masked_apply(p, wide_ref[c], tall_ref[c], keep))
    total = None
    for c in each:
        adjoint_ref[at[c]] = adjoint[c]
        grad_q_ref[at[c]] = adjoint[c].astype(BF16)
        left_high, left_low = split2(rows(grads[c].T, adjoint[c].T))
        high, low = split2(solved_ref[at[c]])
        term = mm(lanes(left_high, left_low, left_high), rows(high, high, low))
        total = term if total is None else total + term
    suffix = total[:D]
    pairs = total[D:] + total[D:].T
    for j in range(XN):
        part_ref[j, :32] = suffix[32 * j : 32 * j + 32]
        part_ref[j, 32:64] = pairs[32 * j : 32 * j + 32]
        part_ref[j, 64:] = jnp.broadcast_to(gain_part, (8, D))


def local_kernel(k_ref, v_ref, solved_ref, adjoint_ref, grad_mixed_ref, grad_k_ref, grad_v_ref):
    chunks = k_ref.shape[0] // C
    keep = iota2(0) <= iota2(1)
    suffix = pairs = None
    for c in reversed(range(chunks)):
        at = slice(C * c, C * c + C)
        k = k_ref[at]
        v = v_ref[at]
        solved, adjoint, grad = solved_ref[at], adjoint_ref[at], grad_mixed_ref[at]
        s_high, s_low = split2(solved)
        a_high, a_low = split2(adjoint)
        g_high, g_low = split2(grad)
        st_high, st_low = split2(solved.T)
        at_high, at_low = split2(adjoint.T)
        gt_high, gt_low = split2(grad.T)
        both = mm(lanes(k, k), rows(lanes(st_high, at_high), lanes(st_low, at_low)))
        value_grad = mm(lanes(v, v), rows(gt_high, gt_low))
        key_solved = jnp.where(keep, both[:, :C], 0.0)
        other = jnp.where(keep, value_grad - both[:, C:], 0.0)
        ks_high, ks_low = split2(key_solved)
        o_high, o_low = split2(other)
        grad_v = mm(lanes(ks_high, ks_low, ks_high), rows(g_high, g_high, g_low))
        grad_k = mm(lanes(o_high, o_low, o_high), rows(s_high, s_high, s_low)) - mm(
            lanes(ks_high, ks_low, ks_high), rows(a_high, a_high, a_low)
        )
        if suffix is not None:
            more_k, more_v = finish(k, v, suffix, pairs)
            grad_k = grad_k + more_k
            grad_v = grad_v + more_v
        grad_k_ref[at] = grad_k
        grad_v_ref[at] = grad_v
        if c > 0:
            left_high, left_low = rows(gt_high, at_high), rows(gt_low, at_low)
            term = mm(lanes(left_high, left_low, left_high), rows(s_high, s_high, s_low))
            pair = term[D:] + term[D:].T
            suffix = term[:D] if suffix is None else suffix + term[:D]
            pairs = pair if pairs is None else pairs + pair


def finish(k, v, suffix, pairs):
    s_high, s_low = split2(suffix)
    p_high, p_low = split2(-pairs)
    t_high, t_low = split2(suffix.T)
    grad_k = mm(lanes(v, v), rows(s_high, s_low)) + mm(lanes(k, k), rows(p_high, p_low))
    return grad_k, mm(lanes(k, k), rows(t_high, t_low))


def last_kernel(k_ref, v_ref, state_ref, local_k_ref, local_v_ref, grad_k_ref, grad_v_ref):
    grad_k, grad_v = finish(k_ref[...], v_ref[...], quarters(state_ref, 0), quarters(state_ref, 32))
    grad_k_ref[...] = (local_k_ref[...] + grad_k).astype(BF16)
    grad_v_ref[...] = (local_v_ref[...] + grad_v).astype(BF16)


def exchange(array, axis):
    return lax.all_to_all(array, axis, split_axis=0, concat_axis=0, tiled=True)


def per_device(queries, keys, values, ridge, gain, grad_out):
    tok = queries.shape[0]
    chunks = tok // C
    z_index = lax.axis_index("z").reshape(1)
    gain_row = gain.reshape(1, D)
    token = (tok, D)

    (parts,) = call(gram_kernel, [((XN, 64, D), F32)], [VMEM] * 2, (keys, values), 4 * tok * D * D)
    parts = exchange(parts, "x")
    (copies,) = call(total_kernel, [((ZN, 64, D), F32)], [VMEM], (parts,), 10**5)
    copies = exchange(copies, "z")
    (state,) = call(before_kernel, [((XN, 64, D), F32)], [SMEM, VMEM, VMEM], (z_index, parts, copies), 10**5)
    state = exchange(state, "x")
    solved, mixed, sums, wide, tall, assoc = call(
        forward_kernel,
        [(token, F32), (token, F32), ((HEADS, 8, D), F32),
         ((chunks, 2 * C, 2 * D), BF16), ((chunks, 3 * C, D), BF16), ((chunks, D, D), F32)],
        [SMEM] + [VMEM] * 6,
        (ridge, queries, keys, values, grad_out, gain_row, state),
        10**9,
    )
    sums = exchange(sums, "head")
    output, grad_q, adjoint, grad_mixed, parts = call(
        adjoint_kernel,
        [(token, BF16), (token, BF16), (token, F32), (token, F32), ((XN, 72, D), F32)],
        [VMEM] * 10,
        (keys, values, grad_out, gain_row, sums, solved, mixed, wide, tall, assoc),
        10**9,
    )
    local_k, local_v = call(
        local_kernel,
        [(token, F32), (token, F32)],
        [VMEM] * 5,
        (keys, values, solved, adjoint, grad_mixed),
        5 * 10**8,
    )
    parts = exchange(parts, "x")
    (copies,) = call(total_kernel, [((ZN, 72, D), F32)], [VMEM], (parts,), 10**5)
    copies = exchange(copies, "z")
    state, grad_gain = call(
        after_kernel, [((XN, 64, D), F32), ((8, D), F32)], [SMEM, VMEM, VMEM], (z_index, parts, copies), 10**5
    )
    state = exchange(state, "x")
    grad_k, grad_v = call(
        last_kernel, [(token, BF16), (token, BF16)], [VMEM] * 5, (keys, values, state, local_k, local_v), 10**8
    )
    return output, grad_q, grad_k, grad_v, grad_gain[0]


def solution(mesh):
    split = Mesh(mesh.devices.reshape(ZN, XN, mesh.shape["head"]), ("z", "x", "head"))
    tokens = P(SEQ, "head")
    return jax.shard_map(
        per_device,
        mesh=split,
        in_specs=(tokens, tokens, tokens, P("head"), P("head"), tokens),
        out_specs=(tokens, tokens, tokens, tokens, P("head")),
        check_vma=False,
    )
```

time: 210 us -> 112 us (0.53)
  blocking collectives: 166 us -> 29.5 us
  Pallas kernels: 0 us -> 28.6 us
  waiting for transfers between devices: 0.01 us -> 28.6 us
  matrix products: 23.3 us -> 0 us
  starting transfers between devices: 7.18 us -> 18.5 us
  other arithmetic: 3.83 us -> 0 us
    all_gather x8 -> x0, blocking collectives: 156 us -> none  [prefix_by_axis(): pieces = jax.tree.map(lambda part: lax.all_gather(part, axis), running)]
    all_to_all x0 -> x3, blocking collectives: none -> 29.5 us  [exchange(): return lax.all_to_all(array, axis, split_axis=0, concat_axis=0, tiled=True)]
    pallas_call x0 -> x9, Pallas kernels: none -> 28.6 us  [call(): pl.pallas_call(kernel, out_shape=[jax.ShapeDtypeStruct(s, t) for s, t in...]
    all_to_all x1 -> x4, waiting for transfers between devices: 0.01 us -> 28.6 us  [exchange(): return lax.all_to_all(array, axis, split_axis=0, concat_axis=0, tiled=True)]
    dot_general x54 -> x0, matrix products: 23.3 us -> none  [the longest x33 14.9 us: matmul(): return jnp.dot(left, right, precision=HIGH)]
    all_to_all x1 -> x4, starting transfers between devices: 7.18 us -> 18.5 us  [exchange(): return lax.all_to_all(array, axis, split_axis=0, concat_axis=0, tiled=True)]
    psum x1 -> x0, blocking collectives: 10 us -> none  [per_device(): squares = lax.psum(jnp.sum(mixed * mixed, axis=(2, 3)), 'head')]
    convert_element_type x3 -> x0, local copies, waits for them, and re-layouts: 2.28 us -> none  [the longest x1 0.76 us: per_device(): grad_values.astype(jnp.bfloat16)]
  transfers between devices with their start and end apart: 1 -> 4, of which waited for: 0 -> 4; matrix products, arithmetic and copies ran while one was open for 8% -> 1% of each run, Pallas kernels for 0% -> 3%
where the time goes in v1:
time: 112 us; the launch traced here: 110 us
  blocking collectives  29.5 us (26%)
  Pallas kernels  28.6 us (26%)
  waiting for transfers between devices  28.6 us (26%)
  starting transfers between devices  18.5 us (17%)
  local copies, waits for them, and re-layouts  3.92 us (4%)
  between operations  1.31 us (1%)
    all_to_all x3, blocking collectives, exchange(): return lax.all_to_all(array, axis, split_axis=0, concat_axis=0, tiled=True)  29.5 us
    pallas_call x9, Pallas kernels, call(): pl.pallas_call(kernel, out_shape=[jax.ShapeDtypeStruct(s, t) for s, t in...  28.6 us
    all_to_all x4, waiting for transfers between devices, exchange(): return lax.all_to_all(array, axis, split_axis=0, concat_axis=0, tiled=True)  28.6 us
    all_to_all x4, starting transfers between devices, exchange(): return lax.all_to_all(array, axis, split_axis=0, concat_axis=0, tiled=True)  18.5 us
    unnamed x8, local copies, waits for them, and re-layouts  2.72 us
  transfers between devices with their start and end apart: 4, of which 4 were waited for; matrix products, arithmetic and copies ran while one was open for 1% of the time, Pallas kernels for 3%

profile of v1, /device:TPU:8, one launch (start us, length us, event | category | flops | bytes accessed | tf_op | source)
XLA Modules:
  0.0 110.5 jit_solution(6548618041448756916)
XLA Ops:
  0.6 1.9 %shard_map.101 = f32[4,64,128]{2,1,0:T(8,128)} custom-call(bf16[512,128]{1,0:T(8,128)(2,1)} %k_ref.9, bf16[512,128]{1,0:T(8,128)(2,1)} %v_ref.9), custom_call_target="tpu_custom_call" | custom-call | flops 33554432 | bytes 262144 | tf_op jit(solution)/shard_map/pallas_call | solution.py:54
  2.5 10.4 %all_to_all.35.a_ref = f32[4,64,128]{2,1,0:T(8,128)} all-to-all(f32[4,64,128]{2,1,0:T(8,128)} %shard_map.101), channel_id=1, replica_groups=mesh['z'=8,'x'=4,'head'=8] {'x'}, dimensions={0} | all-to-all | bytes 262144 | tf_op jit(solution)/shard_map/all_to_all | solution.py:286
  12.9 1.6 %shard_map.102 = f32[8,64,128]{2,1,0:T(8,128)} custom-call(f32[4,64,128]{2,1,0:T(8,128)} %all_to_all.35.a_ref), custom_call_target="tpu_custom_call" | custom-call | flops 100000 | bytes 131072 | tf_op jit(solution)/shard_map/pallas_call | solution.py:54
  14.5 8.5 %all-to-all-start.1 = ((f32[8,64,128]{2,1,0:T(8,128)}), f32[8,64,128]{2,1,0:T(8,128)S(1)}, u32[]{:S(2)}, u32[]{:S(2)}) async-start(f32[8,64,128]{2,1,0:T(8,128)} %shard_map.102), calls=%async_computation.1 | async-start | bytes 524288 | tf_op jit(solution)/shard_map/all_to_all | solution.py:286
  23.0 10.5 %all-to-all-done.1.b_ref = f32[8,64,128]{2,1,0:T(8,128)S(1)} async-done(((f32[8,64,128]{2,1,0:T(8,128)}), f32[8,64,128]{2,1,0:T(8,128)S(1)}, u32[]{:S(2)}, u32[]{:S(2)}) %all-to-all-start.1) | async-done | bytes 262176 | tf_op jit(solution)/shard_map/all_to_all | solution.py:286
  33.5 0.7 copy-done.1
  34.2 1.7 %shard_map.103 = f32[4,64,128]{2,1,0:T(8,128)} custom-call(s32[1]{0:T(128)} %bitcast.1.z_ref, f32[4,64,128]{2,1,0:T(8,128)} %all_to_all.35.a_ref, f32[8,64,128]{2,1,0:T(8,128)} %copy-done.1), custom_call_target="tpu_custom_call" | custom-call | flops 100000 | bytes 393220 | tf_op jit(solution)/shard_map/pallas_call | solution.py:54
  35.9 3.3 %all-to-all-start.2 = ((f32[4,64,128]{2,1,0:T(8,128)}), f32[4,64,128]{2,1,0:T(8,128)S(1)}, u32[]{:S(2)}, u32[]{:S(2)}) async-start(f32[4,64,128]{2,1,0:T(8,128)} %shard_map.103), calls=%async_computation.2 | async-start | bytes 262144 | tf_op jit(solution)/shard_map/all_to_all | solution.py:286
  39.8 5.3 %all-to-all-done.2.state_ref = f32[4,64,128]{2,1,0:T(8,128)S(1)} async-done(((f32[4,64,128]{2,1,0:T(8,128)}), f32[4,64,128]{2,1,0:T(8,128)S(1)}, u32[]{:S(2)}, u32[]{:S(2)}) %all-to-all-start.2) | async-done | bytes 131104 | tf_op jit(solution)/shard_map/all_to_all | solution.py:286
  45.8 7.0 %shard_map.104 = (f32[512,128]{1,0:T(8,128)}, f32[512,128]{1,0:T(8,128)}, f32[8,8,128]{2,1,0:T(8,128)}, bf16[4,256,256]{2,1,0:T(8,128)(2,1)}, bf16[4,384,128]{2,1,0:T(8,128)(2,1)}, /*index=5*/f32[4,128,128]{2,1,0:T(8,128)}) custom-call(f32[1]{0:T(128)S(6)} %copy.11.ridge_ref, bf16[512,128]{1,0:T(8,128)(2,1)} %q_ref.1, bf16[512,128]{1,0:T(8,128)(2,1)} %k_ref.9, ...), custom_call_target="tpu_custom_call" | custom-call | flops 1000000000 | bytes 655876 | tf_op jit(solution)/shard_map/pallas_call | solution.py:54
  52.8 9.0 %all_to_all.36.sums_ref = f32[8,8,128]{2,1,0:T(8,128)} all-to-all(f32[8,8,128]{2,1,0:T(8,128)} %get-tuple-element.22), channel_id=1, replica_groups=mesh['z'=8,'x'=4,'head'=8] {'head'}, dimensions={0} | all-to-all | bytes 65536 | tf_op jit(solution)/shard_map/all_to_all | solution.py:286
  61.8 7.3 %shard_map.105 = (bf16[512,128]{1,0:T(8,128)(2,1)}, bf16[512,128]{1,0:T(8,128)(2,1)}, f32[512,128]{1,0:T(8,128)}, f32[512,128]{1,0:T(8,128)}, f32[4,72,128]{2,1,0:T(8,128)}) custom-call(bf16[512,128]{1,0:T(8,128)(2,1)} %k_ref.9, bf16[512,128]{1,0:T(8,128)(2,1)} %v_ref.9, bf16[512,128]{1,0:T(8,128)(2,1)} %g_ref.3, f32[1,128]{1,0:T(1,128)} %bitcast.5, ...), custom_call_target="tpu_custom_call" | custom-call | flops 1000000000 | bytes 2130432 | tf_op jit(solution)/shard_map/pallas_call | solution.py:54
  69.1 10.1 %all_to_all.37.a_ref = f32[4,72,128]{2,1,0:T(8,128)} all-to-all(f32[4,72,128]{2,1,0:T(8,128)} %get-tuple-element.30), channel_id=1, replica_groups=mesh['z'=8,'x'=4,'head'=8] {'x'}, dimensions={0} | all-to-all | bytes 294912 | tf_op jit(solution)/shard_map/all_to_all | solution.py:286
  79.2 1.6 %shard_map.106 = f32[8,72,128]{2,1,0:T(8,128)} custom-call(f32[4,72,128]{2,1,0:T(8,128)} %all_to_all.37.a_ref), custom_call_target="tpu_custom_call" | custom-call | flops 100000 | bytes 147456 | tf_op jit(solution)/shard_map/pallas_call | solution.py:54
  80.8 3.4 %all-to-all-start.5 = ((f32[8,72,128]{2,1,0:T(8,128)}), f32[8,72,128]{2,1,0:T(8,128)S(1)}, u32[]{:S(2)}, u32[]{:S(2)}) async-start(f32[8,72,128]{2,1,0:T(8,128)} %shard_map.106), calls=%async_computation.5 | async-start | bytes 589824 | tf_op jit(solution)/shard_map/all_to_all | solution.py:286
  84.3 3.5 %shard_map.108 = (f32[512,128]{1,0:T(8,128)}, f32[512,128]{1,0:T(8,128)}) custom-call(bf16[512,128]{1,0:T(8,128)(2,1)} %k_ref.9, bf16[512,128]{1,0:T(8,128)(2,1)} %v_ref.9, f32[512,128]{1,0:T(8,128)} %get-tuple-element.23.solved_ref, f32[512,128]{1,0:T(8,128)} %get-tuple-element.32.adjoint_ref, f32[512,128]{1,0:T(8,128)} %get-tuple-element.33.grad_mixed_ref), custom_call_target="tpu_custom_call" | custom-call | flops 500000000 | bytes 1048576 | tf_op jit(solution)/shard_map/pallas_call | solution.py:54
  87.8 8.1 %all-to-all-done.5.b_ref = f32[8,72,128]{2,1,0:T(8,128)S(1)} async-done(((f32[8,72,128]{2,1,0:T(8,128)}), f32[8,72,128]{2,1,0:T(8,128)S(1)}, u32[]{:S(2)}, u32[]{:S(2)}) %all-to-all-start.5) | async-done | bytes 294944 | tf_op jit(solution)/shard_map/all_to_all | solution.py:286
  95.8 0.7 copy-done
  96.5 1.7 %shard_map.107 = (f32[4,64,128]{2,1,0:T(8,128)}, f32[8,128]{1,0:T(8,128)}) custom-call(s32[1]{0:T(128)} %bitcast.1.z_ref, f32[4,72,128]{2,1,0:T(8,128)} %all_to_all.37.a_ref, f32[8,72,128]{2,1,0:T(8,128)} %copy-done), custom_call_target="tpu_custom_call" | custom-call | flops 100000 | bytes 442372 | tf_op jit(solution)/shard_map/pallas_call | solution.py:54
  98.3 3.3 %all-to-all-start.6 = ((f32[4,64,128]{2,1,0:T(8,128)}), f32[4,64,128]{2,1,0:T(8,128)S(1)}, u32[]{:S(2)}, u32[]{:S(2)}) async-start(f32[4,64,128]{2,1,0:T(8,128)} %get-tuple-element.31), calls=%async_computation.6 | async-start | bytes 262144 | tf_op jit(solution)/shard_map/all_to_all | solution.py:286
  101.6 1.2 %slice_bitcast_fusion = f32[128]{0:T(128)} fusion(f32[8,128]{1,0:T(8,128)} %get-tuple-element.38), kind=kLoop, calls=%fused_computation | loop fusion | bytes 1024 | tf_op jit(solution)/shard_map/squeeze | solution.py:335
  102.8 4.7 %all-to-all-done.6.state_ref = f32[4,64,128]{2,1,0:T(8,128)S(1)} async-done(((f32[4,64,128]{2,1,0:T(8,128)}), f32[4,64,128]{2,1,0:T(8,128)S(1)}, u32[]{:S(2)}, u32[]{:S(2)}) %all-to-all-start.6) | async-done | bytes 131104 | tf_op jit(solution)/shard_map/all_to_all | solution.py:286
  107.5 0.7 copy-done.2
  108.2 2.3 %shard_map.109 = (bf16[512,128]{1,0:T(8,128)(2,1)}, bf16[512,128]{1,0:T(8,128)(2,1)}) custom-call(bf16[512,128]{1,0:T(8,128)(2,1)} %k_ref.9, bf16[512,128]{1,0:T(8,128)(2,1)} %v_ref.9, f32[4,64,128]{2,1,0:T(8,128)} %copy-done.2, f32[512,128]{1,0:T(8,128)} %get-tuple-element.34.local_k_ref, f32[512,128]{1,0:T(8,128)} %get-tuple-element.35.local_v_ref), custom_call_target="tpu_custom_call" | custom-call | flops 100000000 | bytes 917504 | tf_op jit(solution)/shard_map/pallas_call | solution.py:54
  (5 shorter events, 0.7 us)
Async XLA Ops:
  14.5 18.9 %all-to-all-start.1 = ((f32[8,64,128]{2,1,0:T(8,128)}), f32[8,64,128]{2,1,0:T(8,128)S(1)}, u32[]{:S(2)}, u32[]{:S(2)}) async-start(f32[8,64,128]{2,1,0:T(8,128)} %shard_map.102), calls=%async_computation.1 | async-start | bytes 524288 | tf_op jit(solution)/shard_map/all_to_all | solution.py:286
  33.5 0.7 copy-start.1
  35.9 9.3 %all-to-all-start.2 = ((f32[4,64,128]{2,1,0:T(8,128)}), f32[4,64,128]{2,1,0:T(8,128)S(1)}, u32[]{:S(2)}, u32[]{:S(2)}) async-start(f32[4,64,128]{2,1,0:T(8,128)} %shard_map.103), calls=%async_computation.2 | async-start | bytes 262144 | tf_op jit(solution)/shard_map/all_to_all | solution.py:286
  45.1 0.7 copy-start.3
  80.8 15.0 %all-to-all-start.5 = ((f32[8,72,128]{2,1,0:T(8,128)}), f32[8,72,128]{2,1,0:T(8,128)S(1)}, u32[]{:S(2)}, u32[]{:S(2)}) async-start(f32[8,72,128]{2,1,0:T(8,128)} %shard_map.106), calls=%async_computation.5 | async-start | bytes 589824 | tf_op jit(solution)/shard_map/all_to_all | solution.py:286
  95.8 0.7 copy-start
  98.3 9.3 %all-to-all-start.6 = ((f32[4,64,128]{2,1,0:T(8,128)}), f32[4,64,128]{2,1,0:T(8,128)S(1)}, u32[]{:S(2)}, u32[]{:S(2)}) async-start(f32[4,64,128]{2,1,0:T(8,128)} %get-tuple-element.31), calls=%async_computation.6 | async-start | bytes 262144 | tf_op jit(solution)/shard_map/all_to_all | solution.py:286
  107.5 0.7 copy-start.2

commit v2 on v1

--- a/solution.py
+++ b/solution.py
@@ -49,14 +49,14 @@
     return jnp.sum(x, axis=-1, keepdims=True)
 
 
-def call(kernel, outs, ins, args, flops, scratch=()):
+def call(kernel, outs, ins, args, flops, grant=8):
     size = sum(a.size * a.dtype.itemsize for a in args)
     return pl.pallas_call(
         kernel,
         out_shape=[jax.ShapeDtypeStruct(s, t) for s, t in outs],
         in_specs=ins,
         out_specs=[VMEM] * len(outs),
-        scratch_shapes=list(scratch),
+        compiler_params=pltpu.CompilerParams(vmem_limit_bytes=grant * 2**20),
         cost_estimate=pl.CostEstimate(flops=flops, bytes_accessed=size, transcendentals=0),
     )(*args)
 

time: 112 us -> 97.8 us (0.87)
  Pallas kernels: 28.6 us -> 16.3 us
  waiting for transfers between devices: 28.6 us -> 31.3 us
  blocking collectives: 29.5 us -> 27.2 us
  local copies, waits for them, and re-layouts: 3.92 us -> 2.34 us
    pallas_call x9, Pallas kernels: 28.6 us -> 16.3 us  [call(): pl.pallas_call(kernel, out_shape=[jax.ShapeDtypeStruct(s, t) for s, t in...]
    all_to_all x4, waiting for transfers between devices: 28.6 us -> 31.3 us  [exchange(): return lax.all_to_all(array, axis, split_axis=0, concat_axis=0, tiled=True)]
    all_to_all x3, blocking collectives: 29.5 us -> 27.2 us  [exchange(): return lax.all_to_all(array, axis, split_axis=0, concat_axis=0, tiled=True)]
    unnamed x8 -> x14, local copies, waits for them, and re-layouts: 2.72 us -> 1.82 us
  transfers between devices with their start and end apart: 4 -> 4, of which waited for: 4 -> 4; matrix products, arithmetic and copies ran while one was open for 1% -> 1% of each run, Pallas kernels for 3% -> 2%
where the time goes in v2:
time: 97.8 us; the launch traced here: 97.1 us
  waiting for transfers between devices  31.3 us (32%)
  blocking collectives  27.2 us (28%)
  starting transfers between devices  18.7 us (19%)
  Pallas kernels  16.3 us (17%)
  local copies, waits for them, and re-layouts  2.34 us (2%)
  between operations  1.36 us (1%)
    all_to_all x4, waiting for transfers between devices, exchange(): return lax.all_to_all(array, axis, split_axis=0, concat_axis=0, tiled=True)  31.3 us
    all_to_all x3, blocking collectives, exchange(): return lax.all_to_all(array, axis, split_axis=0, concat_axis=0, tiled=True)  27.2 us
    all_to_all x4, starting transfers between devices, exchange(): return lax.all_to_all(array, axis, split_axis=0, concat_axis=0, tiled=True)  18.7 us
    pallas_call x9, Pallas kernels, call(): pl.pallas_call(kernel, out_shape=[jax.ShapeDtypeStruct(s, t) for s, t in...  16.3 us
  transfers between devices with their start and end apart: 4, of which 4 were waited for; matrix products, arithmetic and copies ran while one was open for 1% of the time, Pallas kernels for 2%

profile of v2, /device:TPU:8, one launch (start us, length us, event | category | flops | bytes accessed | tf_op | source)
XLA Modules:
  0.0 97.1 jit_solution(8763122203437156531)
XLA Ops:
  0.6 0.0 copy-start
  0.6 0.9 copy-done
  1.5 0.9 copy-done.2
  2.4 0.3 shard_map.101
  2.7 10.1 %all_to_all.35.a_ref = f32[4,64,128]{2,1,0:T(8,128)S(1)} all-to-all(f32[4,64,128]{2,1,0:T(8,128)S(1)} %shard_map.101), channel_id=1, replica_groups=mesh['z'=8,'x'=4,'head'=8] {'x'}, dimensions={0} | all-to-all | bytes 262144 | tf_op jit(solution)/shard_map/all_to_all | solution.py:286
  12.8 0.7 shard_map.102
  13.5 8.5 %all-to-all-start.1 = ((f32[8,64,128]{2,1,0:T(8,128)}), f32[8,64,128]{2,1,0:T(8,128)S(1)}, u32[]{:S(2)}, u32[]{:S(2)}) async-start(f32[8,64,128]{2,1,0:T(8,128)} %shard_map.102), calls=%async_computation.1 | async-start | bytes 524288 | tf_op jit(solution)/shard_map/all_to_all | solution.py:286
  22.0 10.5 %all-to-all-done.1.b_ref = f32[8,64,128]{2,1,0:T(8,128)S(1)} async-done(((f32[8,64,128]{2,1,0:T(8,128)}), f32[8,64,128]{2,1,0:T(8,128)S(1)}, u32[]{:S(2)}, u32[]{:S(2)}) %all-to-all-start.1) | async-done | bytes 262176 | tf_op jit(solution)/shard_map/all_to_all | solution.py:286
  32.5 0.7 shard_map.103
  33.1 3.5 %all-to-all-start.2 = ((f32[4,64,128]{2,1,0:T(8,128)}), f32[4,64,128]{2,1,0:T(8,128)S(1)}, u32[]{:S(2)}, u32[]{:S(2)}) async-start(f32[4,64,128]{2,1,0:T(8,128)} %shard_map.103), calls=%async_computation.2 | async-start | bytes 262144 | tf_op jit(solution)/shard_map/all_to_all | solution.py:286
  37.3 5.3 %all-to-all-done.2.state_ref = f32[4,64,128]{2,1,0:T(8,128)S(1)} async-done(((f32[4,64,128]{2,1,0:T(8,128)}), f32[4,64,128]{2,1,0:T(8,128)S(1)}, u32[]{:S(2)}, u32[]{:S(2)}) %all-to-all-start.2) | async-done | bytes 131104 | tf_op jit(solution)/shard_map/all_to_all | solution.py:286
  42.6 5.2 %shard_map.104 = (f32[512,128]{1,0:T(8,128)S(1)}, f32[512,128]{1,0:T(8,128)S(1)}, f32[8,8,128]{2,1,0:T(8,128)S(1)}, bf16[4,256,256]{2,1,0:T(8,128)(2,1)S(1)}, bf...) custom-call(f32[1]{0:T(128)S(6)} %copy.11.ridge_ref, bf16[512,128]{1,0:T(8,128)(2,1)S(1)} %copy-done.4, ...), custom_call_target="tpu_custom_call" | custom-call | flops 1000000000 | bytes 655876 | tf_op jit(solution)/shard_map/pallas_call | solution.py:54
  47.8 8.7 %all_to_all.36.sums_ref = f32[8,8,128]{2,1,0:T(8,128)S(1)} all-to-all(f32[8,8,128]{2,1,0:T(8,128)S(1)} %get-tuple-element.22), channel_id=1, replica_groups=mesh['z'=8,'x'=4,'head'=8] {'head'}, dimensions={0} | all-to-all | bytes 65536 | tf_op jit(solution)/shard_map/all_to_all | solution.py:286
  56.5 5.5 %shard_map.105 = (bf16[512,128]{1,0:T(8,128)(2,1)}, bf16[512,128]{1,0:T(8,128)(2,1)}, f32[512,128]{1,0:T(8,128)S(1)}, f32[512,128]{1,0:T(8,128)S(1)}, f32[4,72,128]{2,1,0:T(8,128)S(1)}) custom-call(bf16[512,128]{1,0:T(8,128)(2,1)S(1)} %copy-done.1, bf16[512,128]{1,0:T(8,128)(2,1)S(1)} %copy-done.3, bf16[512,128]{1,0:T(8,128)(2,1)S(1)} %copy-done.5, ...), custom_call_target="tpu_custom_call" | custom-call | flops 1000000000 | bytes 2130432 | tf_op jit(solution)/shard_map/pallas_call | solution.py:54
  61.9 8.4 %all_to_all.37.a_ref = f32[4,72,128]{2,1,0:T(8,128)S(1)} all-to-all(f32[4,72,128]{2,1,0:T(8,128)S(1)} %get-tuple-element.30), channel_id=1, replica_groups=mesh['z'=8,'x'=4,'head'=8] {'x'}, dimensions={0} | all-to-all | bytes 294912 | tf_op jit(solution)/shard_map/all_to_all | solution.py:286
  70.3 0.7 shard_map.106
  71.1 3.4 %all-to-all-start.5 = ((f32[8,72,128]{2,1,0:T(8,128)}), f32[8,72,128]{2,1,0:T(8,128)S(1)}, u32[]{:S(2)}, u32[]{:S(2)}) async-start(f32[8,72,128]{2,1,0:T(8,128)} %shard_map.106), calls=%async_computation.5 | async-start | bytes 589824 | tf_op jit(solution)/shard_map/all_to_all | solution.py:286
  74.5 1.5 %shard_map.108 = (f32[512,128]{1,0:T(8,128)S(1)}, f32[512,128]{1,0:T(8,128)S(1)}) custom-call(bf16[512,128]{1,0:T(8,128)(2,1)S(1)} %copy-done.1, bf16[512,128]{1,0:T(8,128)(2,1)S(1)} %copy-done.3, f32[512,128]{1,0:T(8,128)S(1)} %get-tuple-element.23.solved_ref, f32[512,128]{1,0:T(8,128)S(1)} %get-tuple-element.32.adjoint_ref, ...), custom_call_target="tpu_custom_call" | custom-call | flops 500000000 | bytes 1048576 | tf_op jit(solution)/shard_map/pallas_call | solution.py:54
  76.0 10.1 %all-to-all-done.5.b_ref = f32[8,72,128]{2,1,0:T(8,128)S(1)} async-done(((f32[8,72,128]{2,1,0:T(8,128)}), f32[8,72,128]{2,1,0:T(8,128)S(1)}, u32[]{:S(2)}, u32[]{:S(2)}) %all-to-all-start.5) | async-done | bytes 294944 | tf_op jit(solution)/shard_map/all_to_all | solution.py:286
  86.1 0.7 shard_map.107
  86.7 3.3 %all-to-all-start.6 = ((f32[4,64,128]{2,1,0:T(8,128)}), f32[4,64,128]{2,1,0:T(8,128)S(1)}, u32[]{:S(2)}, u32[]{:S(2)}) async-start(f32[4,64,128]{2,1,0:T(8,128)} %get-tuple-element.31), calls=%async_computation.6 | async-start | bytes 262144 | tf_op jit(solution)/shard_map/all_to_all | solution.py:286
  90.1 0.5 slice_bitcast_fusion
  90.6 5.4 %all-to-all-done.6.state_ref = f32[4,64,128]{2,1,0:T(8,128)S(1)} async-done(((f32[4,64,128]{2,1,0:T(8,128)}), f32[4,64,128]{2,1,0:T(8,128)S(1)}, u32[]{:S(2)}, u32[]{:S(2)}) %all-to-all-start.6) | async-done | bytes 131104 | tf_op jit(solution)/shard_map/all_to_all | solution.py:286
  96.0 1.1 %shard_map.109 = (bf16[512,128]{1,0:T(8,128)(2,1)}, bf16[512,128]{1,0:T(8,128)(2,1)}) custom-call(bf16[512,128]{1,0:T(8,128)(2,1)S(1)} %copy-done.1, bf16[512,128]{1,0:T(8,128)(2,1)S(1)} %copy-done.3, f32[4,64,128]{2,1,0:T(8,128)S(1)} %all-to-all-done.6.state_ref, f32[512,128]{1,0:T(8,128)S(1)} %get-tuple-element.34.local_k_ref, ...), custom_call_target="tpu_custom_call" | custom-call | flops 100000000 | bytes 917504 | tf_op jit(solution)/shard_map/pallas_call | solution.py:54
  (11 shorter events, 0.0 us)
Async XLA Ops:
  0.6 0.9 copy-start
  1.5 0.9 copy-start.2
  13.5 19.0 %all-to-all-start.1 = ((f32[8,64,128]{2,1,0:T(8,128)}), f32[8,64,128]{2,1,0:T(8,128)S(1)}, u32[]{:S(2)}, u32[]{:S(2)}) async-start(f32[8,64,128]{2,1,0:T(8,128)} %shard_map.102), calls=%async_computation.1 | async-start | bytes 524288 | tf_op jit(solution)/shard_map/all_to_all | solution.py:286
  32.5 10.1 %copy-start.4 = (bf16[512,128]{1,0:T(8,128)(2,1)S(1)}, bf16[512,128]{1,0:T(8,128)(2,1)}, u32[]{:S(2)}) copy-start(bf16[512,128]{1,0:T(8,128)(2,1)} %q_ref.1) | copy-start | bytes 393220
  32.5 10.1 %copy-start.5 = (bf16[512,128]{1,0:T(8,128)(2,1)S(1)}, bf16[512,128]{1,0:T(8,128)(2,1)}, u32[]{:S(2)}) copy-start(bf16[512,128]{1,0:T(8,128)(2,1)} %g_ref.3) | copy-start | bytes 393220
  33.1 9.4 %copy-start.1 = (bf16[512,128]{1,0:T(8,128)(2,1)S(1)}, bf16[512,128]{1,0:T(8,128)(2,1)}, u32[]{:S(2)}) copy-start(bf16[512,128]{1,0:T(8,128)(2,1)} %k_ref.9) | copy-start | bytes 393220
  33.1 9.4 %copy-start.3 = (bf16[512,128]{1,0:T(8,128)(2,1)S(1)}, bf16[512,128]{1,0:T(8,128)(2,1)}, u32[]{:S(2)}) copy-start(bf16[512,128]{1,0:T(8,128)(2,1)} %v_ref.9) | copy-start | bytes 393220
  33.1 9.4 %all-to-all-start.2 = ((f32[4,64,128]{2,1,0:T(8,128)}), f32[4,64,128]{2,1,0:T(8,128)S(1)}, u32[]{:S(2)}, u32[]{:S(2)}) async-start(f32[4,64,128]{2,1,0:T(8,128)} %shard_map.103), calls=%async_computation.2 | async-start | bytes 262144 | tf_op jit(solution)/shard_map/all_to_all | solution.py:286
  37.3 5.3 %copy-start.6 = (f32[128]{0:T(128)S(1)}, f32[128]{0:T(128)}, u32[]{:S(2)}) copy-start(f32[128]{0:T(128)} %param.10) | copy-start | bytes 1540
  71.1 15.0 %all-to-all-start.5 = ((f32[8,72,128]{2,1,0:T(8,128)}), f32[8,72,128]{2,1,0:T(8,128)S(1)}, u32[]{:S(2)}, u32[]{:S(2)}) async-start(f32[8,72,128]{2,1,0:T(8,128)} %shard_map.106), calls=%async_computation.5 | async-start | bytes 589824 | tf_op jit(solution)/shard_map/all_to_all | solution.py:286
  86.7 9.3 %all-to-all-start.6 = ((f32[4,64,128]{2,1,0:T(8,128)}), f32[4,64,128]{2,1,0:T(8,128)S(1)}, u32[]{:S(2)}, u32[]{:S(2)}) async-start(f32[4,64,128]{2,1,0:T(8,128)} %get-tuple-element.31), calls=%async_computation.6 | async-start | bytes 262144 | tf_op jit(solution)/shard_map/all_to_all | solution.py:286

commit v3 on v1

--- a/solution.py
+++ b/solution.py
@@ -12,12 +12,14 @@
 EPS = 1e-06
 ZN = 8
 XN = 4
+SLICES = ZN * XN
+GAIN_SLICE = 25
 SEQ = ("z", "x")
 C = 128
 F32 = jnp.float32
 BF16 = jnp.bfloat16
 VMEM = pl.BlockSpec(memory_space=pltpu.VMEM)
-SMEM = pl.BlockSpec(memory_space=pltpu.SMEM)
+HBM = pl.BlockSpec(memory_space=pltpu.HBM)
 
 
 def split2(x):
@@ -49,7 +51,7 @@
     return jnp.sum(x, axis=-1, keepdims=True)
 
 
-def call(kernel, outs, ins, args, flops, scratch=()):
+def call(kernel, outs, ins, args, flops, grant=8192, scratch=()):
     size = sum(a.size * a.dtype.itemsize for a in args)
     return pl.pallas_call(
         kernel,
@@ -57,6 +59,7 @@
         in_specs=ins,
         out_specs=[VMEM] * len(outs),
         scratch_shapes=list(scratch),
+        compiler_params=pltpu.CompilerParams(vmem_limit_bytes=grant * 2**10),
         cost_estimate=pl.CostEstimate(flops=flops, bytes_accessed=size, transcendentals=0),
     )(*args)
 
@@ -89,48 +92,50 @@
     return sol
 
 
-def gram_kernel(k_ref, v_ref, out_ref):
+def gram_kernel(k_hbm, v_hbm, out_ref, k_ref, v_ref, sem):
+    copies = [
+        pltpu.make_async_copy(k_hbm, k_ref, sem.at[0]),
+        pltpu.make_async_copy(v_hbm, v_ref, sem.at[1]),
+    ]
+    for copy in copies:
+        copy.start()
+    for copy in copies:
+        copy.wait()
     k = k_ref[...]
-    both = mm_t(lanes(k, v_ref[...]), k)
-    for j in range(XN):
-        out_ref[j, :32] = both[32 * j : 32 * j + 32]
-        out_ref[j, 32:] = both[D + 32 * j : D + 32 * j + 32]
-
-
-def total_kernel(a_ref, out_ref):
-    total = a_ref[0] + a_ref[1] + a_ref[2] + a_ref[3]
-    for z in range(ZN):
-        out_ref[z] = total
-
-
-def before_kernel(z_ref, a_ref, b_ref, out_ref):
-    z = z_ref[0]
-    run = jnp.where(z > 0, b_ref[0], 0.0)
-    for k in range(1, ZN - 1):
-        run = run + jnp.where(k < z, b_ref[k], 0.0)
-    for j in range(XN):
-        out_ref[j] = run
-        if j < XN - 1:
-            run = run + a_ref[j]
-
-
-def after_kernel(z_ref, a_ref, b_ref, out_ref, gain_ref):
-    z = z_ref[0]
-    run = jnp.where(z < ZN - 1, b_ref[ZN - 1, :64], 0.0)
-    for k in range(1, ZN - 1):
-        run = run + jnp.where(k > z, b_ref[k, :64], 0.0)
-    for j in reversed(range(XN)):
-        out_ref[j] = run
-        if j > 0:
-            run = run + a_ref[j, :64]
-    gain = b_ref[0, 64:]
-    for k in range(1, ZN):
-        gain = gain + b_ref[k, 64:]
-    gain_ref[...] = gain
-
-
-def quarters(ref, start):
-    return rows(*[ref[j, start : start + 32] for j in range(XN)])
+    out_ref[...] = mm_t(lanes(k, v_ref[...]), k)
+
+
+def before_kernel(a_ref, out_ref):
+    run = jnp.zeros((8, D), F32)
+    for k in range(SLICES):
+        out_ref[k] = run
+        run = run + a_ref[k]
+
+
+def after_kernel(a_ref, out_ref):
+    total = a_ref[0]
+    for k in range(1, SLICES):
+        total = total + a_ref[k]
+    whole = lax.axis_index("z") * XN + lax.axis_index("x") == GAIN_SLICE
+    run = jnp.zeros((8, D), F32)
+    for k in reversed(range(SLICES)):
+        out_ref[k] = jnp.where(whole, total, run)
+        run = run + a_ref[k]
+
+
+def pack(pairs):
+    row = lax.broadcasted_iota(jnp.int32, (C // 2, C), 0)
+    col = lax.broadcasted_iota(jnp.int32, (C // 2, C), 1)
+    turned = pltpu.roll(pairs[C // 2 :], C // 2, 1)
+    return jnp.where((col < C // 2) & (col > row), turned, pairs[: C // 2])
+
+
+def unpack(packed, diagonal):
+    row, col = iota2(0), iota2(1)
+    half = C // 2
+    both = rows(packed, pltpu.roll(packed, half, 1))
+    direct = ((row < half) & ((col >= half) | (row >= col))) | ((row >= half) & (col >= half) & (row < col))
+    return jnp.where(row == col, diagonal, jnp.where(direct, both, both.T))
 
 
 def forward_kernel(ridge_ref, q_ref, k_ref, v_ref, g_ref, gain_ref, state_ref,
@@ -140,8 +145,8 @@
     at = [slice(C * c, C * c + C) for c in each]
     keep = iota2(0) >= iota2(1)
     eye = iota2(0) == iota2(1)
-    gram = quarters(state_ref, 0) + jnp.where(eye, ridge_ref[0], 0.0)
-    assoc = quarters(state_ref, 32)
+    gram = state_ref[:D] + jnp.where(eye, ridge_ref[...], 0.0)
+    assoc = state_ref[D:]
     turned = []
     for c in each:
         k = k_ref[at[c]]
@@ -194,7 +199,7 @@
         sums = sums + sums_ref[h]
     columns = rows(sums, jnp.zeros((C - 8, C), F32)).T
     rhs = []
-    gain_part = jnp.zeros((1, D), F32)
+    gain_part = jnp.zeros((8, D), F32)
     grads = []
     for c in each:
         denom = jnp.sqrt(columns[:, c : c + 1] / (HEADS * D) + EPS)
@@ -204,7 +209,7 @@
         scaled = mixed * inverse
         upstream = g_ref[at[c]].astype(F32)
         out_ref[at[c]] = (scaled * gain).astype(BF16)
-        gain_part = gain_part + jnp.sum(upstream * scaled, axis=0, keepdims=True)
+        gain_part = gain_part + jnp.sum((upstream * scaled).reshape(C // 8, 8, D), axis=0)
         grad = gain * upstream * inverse - mixed * factor
         grads.append(grad)
         grad_mixed_ref[at[c]] = grad
@@ -221,12 +226,13 @@
         high, low = split2(solved_ref[at[c]])
         term = mm(lanes(left_high, left_low, left_high), rows(high, high, low))
         total = term if total is None else total + term
-    suffix = total[:D]
     pairs = total[D:] + total[D:].T
-    for j in range(XN):
-        part_ref[j, :32] = suffix[32 * j : 32 * j + 32]
-        part_ref[j, 32:64] = pairs[32 * j : 32 * j + 32]
-        part_ref[j, 64:] = jnp.broadcast_to(gain_part, (8, D))
+    part_ref[:D] = total[:D]
+    part_ref[D : D + 64] = pack(pairs)
+    diagonal = jnp.sum(jnp.where(iota2(0) == iota2(1), pairs, 0.0), axis=0, keepdims=True)
+    part_ref[D + 64 : D + 72] = jnp.broadcast_to(diagonal, (8, D))
+    part_ref[D + 72 : D + 80] = gain_part
+    part_ref[D + 80 :] = jnp.zeros((D - 80, D), F32)
 
 
 def local_kernel(k_ref, v_ref, solved_ref, adjoint_ref, grad_mixed_ref, grad_k_ref, grad_v_ref):
@@ -276,41 +282,51 @@
     return grad_k, mm(lanes(k, k), rows(t_high, t_low))
 
 
-def last_kernel(k_ref, v_ref, state_ref, local_k_ref, local_v_ref, grad_k_ref, grad_v_ref):
-    grad_k, grad_v = finish(k_ref[...], v_ref[...], quarters(state_ref, 0), quarters(state_ref, 32))
+def last_kernel(k_ref, v_ref, state_ref, local_k_ref, local_v_ref, grad_k_ref, grad_v_ref, gain_ref):
+    pairs = unpack(state_ref[D : D + 64], state_ref[D + 64 : D + 65])
+    grad_k, grad_v = finish(k_ref[...], v_ref[...], state_ref[:D], pairs)
     grad_k_ref[...] = (local_k_ref[...] + grad_k).astype(BF16)
     grad_v_ref[...] = (local_v_ref[...] + grad_v).astype(BF16)
+    gain_ref[...] = jnp.sum(state_ref[D + 72 : D + 80], axis=0, keepdims=True)
 
 
 def exchange(array, axis):
     return lax.all_to_all(array, axis, split_axis=0, concat_axis=0, tiled=True)
+
+
+def scan_over_seq(kernel, parts):
+    slices = (SLICES, 8, D)
+    held = exchange(parts.reshape(slices), SEQ)
+    (held,) = call(kernel, [(slices, F32)], [VMEM], (held,), 10**5)
+    return exchange(held, SEQ).reshape(2 * D, D)
 
 
 def per_device(queries, keys, values, ridge, gain, grad_out):
     tok = queries.shape[0]
     chunks = tok // C
-    z_index = lax.axis_index("z").reshape(1)
     gain_row = gain.reshape(1, D)
     token = (tok, D)
-
-    (parts,) = call(gram_kernel, [((XN, 64, D), F32)], [VMEM] * 2, (keys, values), 4 * tok * D * D)
-    parts = exchange(parts, "x")
-    (copies,) = call(total_kernel, [((ZN, 64, D), F32)], [VMEM], (parts,), 10**5)
-    copies = exchange(copies, "z")
-    (state,) = call(before_kernel, [((XN, 64, D), F32)], [SMEM, VMEM, VMEM], (z_index, parts, copies), 10**5)
-    state = exchange(state, "x")
+    state_shape = ((2 * D, D), F32)
+
+    (parts,) = call(
+        gram_kernel, [state_shape], [HBM] * 2, (keys, values), 4 * tok * D * D, grant=55000,
+        scratch=[pltpu.VMEM(token, BF16), pltpu.VMEM(token, BF16), pltpu.SemaphoreType.DMA((2,))],
+    )
+    ridge_row = jnp.broadcast_to(ridge.reshape(1, 1), (1, D))
+    parts, ridge_row = lax.optimization_barrier((parts, ridge_row))
+    state = scan_over_seq(before_kernel, parts)
     solved, mixed, sums, wide, tall, assoc = call(
         forward_kernel,
         [(token, F32), (token, F32), ((HEADS, 8, D), F32),
          ((chunks, 2 * C, 2 * D), BF16), ((chunks, 3 * C, D), BF16), ((chunks, D, D), F32)],
-        [SMEM] + [VMEM] * 6,
-        (ridge, queries, keys, values, grad_out, gain_row, state),
+        [VMEM] * 7,
+        (ridge_row, queries, keys, values, grad_out, gain_row, state),
         10**9,
     )
     sums = exchange(sums, "head")
     output, grad_q, adjoint, grad_mixed, parts = call(
         adjoint_kernel,
-        [(token, BF16), (token, BF16), (token, F32), (token, F32), ((XN, 72, D), F32)],
+        [(token, BF16), (token, BF16), (token, F32), (token, F32), state_shape],
         [VMEM] * 10,
         (keys, values, grad_out, gain_row, sums, solved, mixed, wide, tall, assoc),
         10**9,
@@ -322,17 +338,12 @@
         (keys, values, solved, adjoint, grad_mixed),
         5 * 10**8,
     )
-    parts = exchange(parts, "x")
-    (copies,) = call(total_kernel, [((ZN, 72, D), F32)], [VMEM], (parts,), 10**5)
-    copies = exchange(copies, "z")
-    state, grad_gain = call(
-        after_kernel, [((XN, 64, D), F32), ((8, D), F32)], [SMEM, VMEM, VMEM], (z_index, parts, copies), 10**5
-    )
-    state = exchange(state, "x")
-    grad_k, grad_v = call(
-        last_kernel, [(token, BF16), (token, BF16)], [VMEM] * 5, (keys, values, state, local_k, local_v), 10**8
-    )
-    return output, grad_q, grad_k, grad_v, grad_gain[0]
+    state = scan_over_seq(after_kernel, parts)
+    grad_k, grad_v, grad_gain = call(
+        last_kernel, [(token, BF16), (token, BF16), ((1, D), F32)], [VMEM] * 5,
+        (keys, values, state, local_k, local_v), 10**8,
+    )
+    return output, grad_q, grad_k, grad_v, grad_gain.reshape(D)
 
 
 def solution(mesh):

time: 112 us -> 88.5 us (0.79); the launches traced: 110 us -> 88.2 us
  blocking collectives: 29.5 us -> 57.9 us
  waiting for transfers between devices: 28.6 us -> 9.09 us
  starting transfers between devices: 18.5 us -> 3.86 us
  Pallas kernels: 28.6 us -> 15.3 us
  local copies, waits for them, and re-layouts: 3.92 us -> 0.65 us
    all_to_all x3 -> x4, blocking collectives: 29.5 us -> 57.9 us  [exchange(): return lax.all_to_all(array, axis, split_axis=0, concat_axis=0, tiled=True)]
    all_to_all x4 -> x1, waiting for transfers between devices: 28.6 us -> 9.09 us  [exchange(): return lax.all_to_all(array, axis, split_axis=0, concat_axis=0, tiled=True)]
    all_to_all x4 -> x1, starting transfers between devices: 18.5 us -> 3.86 us  [exchange(): return lax.all_to_all(array, axis, split_axis=0, concat_axis=0, tiled=True)]
    pallas_call x9 -> x7, Pallas kernels: 28.6 us -> 15.3 us  [call(): pl.pallas_call(kernel, out_shape=[jax.ShapeDtypeStruct(s, t) for s, t in...]
    unnamed x8 -> x10, local copies, waits for them, and re-layouts: 2.72 us -> 0.65 us
    squeeze x1 -> x0, local copies, waits for them, and re-layouts: 1.2 us -> none  [per_device(): return (output, grad_q, grad_k, grad_v, grad_gain[0])]
  transfers between devices with their start and end apart: 4 -> 1, of which waited for: 4 -> 1; matrix products, arithmetic and copies ran while one was open for 1% -> 0% of each run, Pallas kernels for 3% -> 2%
where the time goes in v3:
time: 88.5 us; the launch traced here: 88.2 us
  blocking collectives  57.9 us (65%)
  Pallas kernels  15.3 us (17%)
  waiting for transfers between devices  9.09 us (10%)
  starting transfers between devices  3.86 us (4%)
  between operations  1.34 us (2%)
    all_to_all x4, blocking collectives, exchange(): return lax.all_to_all(array, axis, split_axis=0, concat_axis=0, tiled=True)  57.9 us
    pallas_call x7, Pallas kernels, call(): pl.pallas_call(kernel, out_shape=[jax.ShapeDtypeStruct(s, t) for s, t in...  15.3 us
    all_to_all x1, waiting for transfers between devices, exchange(): return lax.all_to_all(array, axis, split_axis=0, concat_axis=0, tiled=True)  9.09 us
    all_to_all x1, starting transfers between devices, exchange(): return lax.all_to_all(array, axis, split_axis=0, concat_axis=0, tiled=True)  3.86 us
  transfers between devices with their start and end apart: 1, of which 1 were waited for; matrix products, arithmetic and copies ran while one was open for 0% of the time, Pallas kernels for 2%

profile of v3, /device:TPU:8, one launch (start us, length us, event | category | flops | bytes accessed | tf_op | source)
XLA Modules:
  0.0 88.2 jit_solution(12807557665449589446)
XLA Ops:
  1.3 1.3 %shard_map.101 = f32[256,128]{1,0:T(8,128)S(1)} custom-call(bf16[512,128]{1,0:T(8,128)(2,1)} %k_ref.7, bf16[512,128]{1,0:T(8,128)(2,1)} %v_ref.7), custom_call_target="tpu_custom_call" | custom-call | flops 33554432 | bytes 262144 | tf_op jit(solution)/shard_map/pallas_call | solution.py:56
  2.6 21.6 %all_to_all.25.a_ref = f32[32,8,128]{2,1,0:T(8,128)S(1)} all-to-all(f32[32,8,128]{2,1,0:T(8,128)S(1)} %bitcast.9), channel_id=1, replica_groups=mesh['z'=8,'x'=4,'head'=8] {'z','x'}, dimensions={0} | all-to-all | bytes 262144 | tf_op jit(solution)/shard_map/all_to_all | solution.py:294
  24.2 0.0 copy-start.2
  24.2 0.0 copy-start.3
  24.2 0.0 copy-start
  24.2 0.0 copy-start.1
  24.2 14.0 %all_to_all.26 = f32[32,8,128]{2,1,0:T(8,128)S(1)} all-to-all(f32[32,8,128]{2,1,0:T(8,128)S(1)} %shard_map.102), channel_id=1, replica_groups=mesh['z'=8,'x'=4,'head'=8] {'z','x'}, dimensions={0} | all-to-all | bytes 262144 | tf_op jit(solution)/shard_map/all_to_all | solution.py:294
  38.2 0.0 copy-start.4
  38.2 0.0 copy-done.2
  38.2 0.0 copy-done.3
  38.2 0.0 copy-done
  38.2 0.0 copy-done.1
  38.3 0.6 copy-done.4
  38.9 5.2 %shard_map.103 = (f32[512,128]{1,0:T(8,128)S(1)}, f32[512,128]{1,0:T(8,128)S(1)}, f32[8,8,128]{2,1,0:T(8,128)S(1)}, bf16[4,256,256]{2,1,0:T(8,128)(2,1)S(1)}, bf...) custom-call(f32[1,128]{1,0:T(1,128)S(1)} %broadcast_in_dim.8.ridge_ref, bf16[512,128]{1,0:T(8,128)(2,1)S(1)} %copy-done.2, ...), custom_call_target="tpu_custom_call" | custom-call | flops 1000000000 | bytes 656384 | tf_op jit(solution)/shard_map/pallas_call | solution.py:56
  44.0 8.7 %all_to_all.27.sums_ref = f32[8,8,128]{2,1,0:T(8,128)S(1)} all-to-all(f32[8,8,128]{2,1,0:T(8,128)S(1)} %get-tuple-element.25), channel_id=1, replica_groups=mesh['z'=8,'x'=4,'head'=8] {'head'}, dimensions={0} | all-to-all | bytes 65536 | tf_op jit(solution)/shard_map/all_to_all | solution.py:294
  52.7 5.4 %shard_map.104 = (bf16[512,128]{1,0:T(8,128)(2,1)}, bf16[512,128]{1,0:T(8,128)(2,1)}, f32[512,128]{1,0:T(8,128)S(1)}, f32[512,128]{1,0:T(8,128)S(1)}, f32[256,128]{1,0:T(8,128)S(1)}) custom-call(bf16[512,128]{1,0:T(8,128)(2,1)S(1)} %copy-done, bf16[512,128]{1,0:T(8,128)(2,1)S(1)} %copy-done.1, bf16[512,128]{1,0:T(8,128)(2,1)S(1)} %copy-done.3, ...), custom_call_target="tpu_custom_call" | custom-call | flops 1000000000 | bytes 2130432 | tf_op jit(solution)/shard_map/pallas_call | solution.py:56
  58.2 13.6 %all_to_all.28.a_ref = f32[32,8,128]{2,1,0:T(8,128)S(1)} all-to-all(f32[32,8,128]{2,1,0:T(8,128)S(1)} %bitcast.10), channel_id=1, replica_groups=mesh['z'=8,'x'=4,'head'=8] {'z','x'}, dimensions={0} | all-to-all | bytes 262144 | tf_op jit(solution)/shard_map/all_to_all | solution.py:294
  71.8 0.7 shard_map.105
  72.5 3.9 %all-to-all-start.4 = ((f32[32,8,128]{2,1,0:T(8,128)}), f32[32,8,128]{2,1,0:T(8,128)S(1)}, u32[]{:S(2)}, u32[]{:S(2)}) async-start(f32[32,8,128]{2,1,0:T(8,128)} %shard_map.105), calls=%async_computation.4 | async-start | bytes 262144 | tf_op jit(solution)/shard_map/all_to_all | solution.py:294
  76.4 1.5 %shard_map.106 = (f32[512,128]{1,0:T(8,128)S(1)}, f32[512,128]{1,0:T(8,128)S(1)}) custom-call(bf16[512,128]{1,0:T(8,128)(2,1)S(1)} %copy-done, bf16[512,128]{1,0:T(8,128)(2,1)S(1)} %copy-done.1, f32[512,128]{1,0:T(8,128)S(1)} %get-tuple-element.26.solved_ref, f32[512,128]{1,0:T(8,128)S(1)} %get-tuple-element.34.adjoint_ref, ...), custom_call_target="tpu_custom_call" | custom-call | flops 500000000 | bytes 1048576 | tf_op jit(solution)/shard_map/pallas_call | solution.py:56
  77.9 9.1 %all-to-all-done.4 = f32[32,8,128]{2,1,0:T(8,128)S(1)} async-done(((f32[32,8,128]{2,1,0:T(8,128)}), f32[32,8,128]{2,1,0:T(8,128)S(1)}, u32[]{:S(2)}, u32[]{:S(2)}) %all-to-all-start.4) | async-done | bytes 131104 | tf_op jit(solution)/shard_map/all_to_all | solution.py:294
  87.0 1.2 %shard_map.107 = (bf16[512,128]{1,0:T(8,128)(2,1)}, bf16[512,128]{1,0:T(8,128)(2,1)}, f32[1,128]{1,0:T(1,128)}) custom-call(bf16[512,128]{1,0:T(8,128)(2,1)S(1)} %copy-done, bf16[512,128]{1,0:T(8,128)(2,1)S(1)} %copy-done.1, f32[256,128]{1,0:T(8,128)S(1)} %bitcast.8, f32[512,128]{1,0:T(8,128)S(1)} %get-tuple-element.36.local_k_ref, ...), custom_call_target="tpu_custom_call" | custom-call | flops 100000000 | bytes 917504 | tf_op jit(solution)/shard_map/pallas_call | solution.py:56
  (2 shorter events, 0.0 us)
Async XLA Ops:
  24.2 14.1 %copy-start.2 = (bf16[512,128]{1,0:T(8,128)(2,1)S(1)}, bf16[512,128]{1,0:T(8,128)(2,1)}, u32[]{:S(2)}) copy-start(bf16[512,128]{1,0:T(8,128)(2,1)} %q_ref.1) | copy-start | bytes 393220
  24.2 14.1 %copy-start.3 = (bf16[512,128]{1,0:T(8,128)(2,1)S(1)}, bf16[512,128]{1,0:T(8,128)(2,1)}, u32[]{:S(2)}) copy-start(bf16[512,128]{1,0:T(8,128)(2,1)} %g_ref.3) | copy-start | bytes 393220
  24.2 14.0 %copy-start = (bf16[512,128]{1,0:T(8,128)(2,1)S(1)}, bf16[512,128]{1,0:T(8,128)(2,1)}, u32[]{:S(2)}) copy-start(bf16[512,128]{1,0:T(8,128)(2,1)} %k_ref.7) | copy-start | bytes 393220
  24.2 14.0 %copy-start.1 = (bf16[512,128]{1,0:T(8,128)(2,1)S(1)}, bf16[512,128]{1,0:T(8,128)(2,1)}, u32[]{:S(2)}) copy-start(bf16[512,128]{1,0:T(8,128)(2,1)} %v_ref.7) | copy-start | bytes 393220
  38.2 0.7 copy-start.4
  72.5 14.5 %all-to-all-start.4 = ((f32[32,8,128]{2,1,0:T(8,128)}), f32[32,8,128]{2,1,0:T(8,128)S(1)}, u32[]{:S(2)}, u32[]{:S(2)}) async-start(f32[32,8,128]{2,1,0:T(8,128)} %shard_map.105), calls=%async_computation.4 | async-start | bytes 262144 | tf_op jit(solution)/shard_map/all_to_all | solution.py:294

commit v4 on v3

--- a/solution.py
+++ b/solution.py
@@ -51,13 +51,13 @@
     return jnp.sum(x, axis=-1, keepdims=True)
 
 
-def call(kernel, outs, ins, args, flops, grant=8192, scratch=()):
+def call(kernel, outs, ins, args, flops, grant=8192, scratch=(), places=None):
     size = sum(a.size * a.dtype.itemsize for a in args)
     return pl.pallas_call(
         kernel,
         out_shape=[jax.ShapeDtypeStruct(s, t) for s, t in outs],
         in_specs=ins,
-        out_specs=[VMEM] * len(outs),
+        out_specs=places or [VMEM] * len(outs),
         scratch_shapes=list(scratch),
         compiler_params=pltpu.CompilerParams(vmem_limit_bytes=grant * 2**10),
         cost_estimate=pl.CostEstimate(flops=flops, bytes_accessed=size, transcendentals=0),
@@ -93,16 +93,23 @@
 
 
 def gram_kernel(k_hbm, v_hbm, out_ref, k_ref, v_ref, sem):
+    half = k_hbm.shape[0] // 2
+    at = [pl.ds(half * n, half) for n in range(2)]
     copies = [
-        pltpu.make_async_copy(k_hbm, k_ref, sem.at[0]),
-        pltpu.make_async_copy(v_hbm, v_ref, sem.at[1]),
+        pltpu.make_async_copy(source.at[at[n]], target.at[at[n]], sem.at[n, m])
+        for n in range(2)
+        for m, (source, target) in enumerate(((k_hbm, k_ref), (v_hbm, v_ref)))
     ]
     for copy in copies:
         copy.start()
-    for copy in copies:
-        copy.wait()
-    k = k_ref[...]
-    out_ref[...] = mm_t(lanes(k, v_ref[...]), k)
+    total = None
+    for n in range(2):
+        copies[2 * n].wait()
+        copies[2 * n + 1].wait()
+        k = k_ref[at[n]]
+        term = mm_t(lanes(k, v_ref[at[n]]), k)
+        total = term if total is None else total + term
+    out_ref[...] = total
 
 
 def before_kernel(a_ref, out_ref):
@@ -138,7 +145,7 @@
     return jnp.where(row == col, diagonal, jnp.where(direct, both, both.T))
 
 
-def forward_kernel(ridge_ref, q_ref, k_ref, v_ref, g_ref, gain_ref, state_ref,
+def forward_kernel(ridge_ref, gain_ref, q_ref, k_ref, v_ref, g_ref, state_ref,
                    solved_ref, mixed_ref, sums_ref, wide_ref, tall_ref, assoc_ref):
     chunks = q_ref.shape[0] // C
     each = range(chunks)
@@ -187,8 +194,8 @@
                 sums_ref[h, row : row + 1] = total[:1]
 
 
-def adjoint_kernel(k_ref, v_ref, g_ref, gain_ref, sums_ref, solved_ref, mixed_ref, wide_ref, tall_ref, assoc_ref,
-                   out_ref, grad_q_ref, adjoint_ref, grad_mixed_ref, part_ref):
+def adjoint_kernel(gain_ref, k_ref, v_ref, g_ref, sums_ref, solved_ref, mixed_ref, wide_ref, tall_ref, assoc_ref,
+                   out_ref, adjoint_ref, grad_mixed_ref, part_ref):
     chunks = k_ref.shape[0] // C
     each = range(chunks)
     at = [slice(C * c, C * c + C) for c in each]
@@ -217,25 +224,30 @@
         high, low = split2(assoc_ref[c])
         top = lanes(v_ref[at[c]].T, high)
         rhs.append(masked_apply(grad, rows(top, top), rows(k, k, low), keep))
+    turned = []
+    for c in each:
+        high, low = split2(solved_ref[at[c]].T)
+        turned.append(lanes(high, low, high))
+    part_ref[D + 72 : D + 80] = gain_part
+    part_ref[D + 80 :] = jnp.zeros((D - 80, D), F32)
     adjoint = conjugate(rhs, lambda c, p: masked_apply(p, wide_ref[c], tall_ref[c], keep))
     total = None
     for c in each:
         adjoint_ref[at[c]] = adjoint[c]
-        grad_q_ref[at[c]] = adjoint[c].astype(BF16)
-        left_high, left_low = split2(rows(grads[c].T, adjoint[c].T))
-        high, low = split2(solved_ref[at[c]])
-        term = mm(lanes(left_high, left_low, left_high), rows(high, high, low))
+        high, low = split2(lanes(grads[c], adjoint[c]))
+        term = mm(turned[c], rows(high, high, low))
         total = term if total is None else total + term
-    pairs = total[D:] + total[D:].T
-    part_ref[:D] = total[:D]
+    part_ref[:D] = total[:, :D].T
+    pairs = total[:, D:] + total[:, D:].T
     part_ref[D : D + 64] = pack(pairs)
     diagonal = jnp.sum(jnp.where(iota2(0) == iota2(1), pairs, 0.0), axis=0, keepdims=True)
     part_ref[D + 64 : D + 72] = jnp.broadcast_to(diagonal, (8, D))
-    part_ref[D + 72 : D + 80] = gain_part
-    part_ref[D + 80 :] = jnp.zeros((D - 80, D), F32)
-
-
-def local_kernel(k_ref, v_ref, solved_ref, adjoint_ref, grad_mixed_ref, grad_k_ref, grad_v_ref):
+
+
+def local_kernel(k_ref, v_ref, solved_ref, adjoint_ref, grad_mixed_ref, scaled_ref,
+                 grad_k_ref, grad_v_ref, out_ref, grad_q_ref):
+    out_ref[...] = scaled_ref[...]
+    grad_q_ref[...] = adjoint_ref[...].astype(BF16)
     chunks = k_ref.shape[0] // C
     keep = iota2(0) <= iota2(1)
     suffix = pairs = None
@@ -274,20 +286,39 @@
             pairs = pair if pairs is None else pairs + pair
 
 
+def key_weights(suffix, pairs):
+    return rows(*split2(suffix), *split2(-pairs))
+
+
 def finish(k, v, suffix, pairs):
-    s_high, s_low = split2(suffix)
-    p_high, p_low = split2(-pairs)
     t_high, t_low = split2(suffix.T)
-    grad_k = mm(lanes(v, v), rows(s_high, s_low)) + mm(lanes(k, k), rows(p_high, p_low))
-    return grad_k, mm(lanes(k, k), rows(t_high, t_low))
-
-
-def last_kernel(k_ref, v_ref, state_ref, local_k_ref, local_v_ref, grad_k_ref, grad_v_ref, gain_ref):
+    return mm(lanes(v, v, k, k), key_weights(suffix, pairs)), mm(lanes(k, k), rows(t_high, t_low))
+
+
+def last_kernel(k_ref, v_ref, state_ref, local_k_ref, local_v_ref, grad_k_hbm, grad_v_hbm, gain_ref,
+                grad_k_ref, grad_v_ref, sem):
+    suffix = state_ref[:D]
     pairs = unpack(state_ref[D : D + 64], state_ref[D + 64 : D + 65])
-    grad_k, grad_v = finish(k_ref[...], v_ref[...], state_ref[:D], pairs)
-    grad_k_ref[...] = (local_k_ref[...] + grad_k).astype(BF16)
-    grad_v_ref[...] = (local_v_ref[...] + grad_v).astype(BF16)
+    half = k_ref.shape[0] // 2
+    copies = []
+    t_high, t_low = split2(suffix.T)
+    turned = rows(t_high, t_low)
+    direct = key_weights(suffix, pairs)
+    for n in range(2):
+        at = pl.ds(half * n, half)
+        k = k_ref[at]
+        grad_v_ref[at] = (local_v_ref[at] + mm(lanes(k, k), turned)).astype(BF16)
+        copies.append(pltpu.make_async_copy(grad_v_ref.at[at], grad_v_hbm.at[at], sem.at[n, 0]))
+        copies[-1].start()
+    for n in range(2):
+        at = pl.ds(half * n, half)
+        k, v = k_ref[at], v_ref[at]
+        grad_k_ref[at] = (local_k_ref[at] + mm(lanes(v, v, k, k), direct)).astype(BF16)
+        copies.append(pltpu.make_async_copy(grad_k_ref.at[at], grad_k_hbm.at[at], sem.at[n, 1]))
+        copies[-1].start()
     gain_ref[...] = jnp.sum(state_ref[D + 72 : D + 80], axis=0, keepdims=True)
+    for copy in copies:
+        copy.wait()
 
 
 def exchange(array, axis):
@@ -304,13 +335,13 @@
 def per_device(queries, keys, values, ridge, gain, grad_out):
     tok = queries.shape[0]
     chunks = tok // C
-    gain_row = gain.reshape(1, D)
     token = (tok, D)
     state_shape = ((2 * D, D), F32)
 
+    gain_row = gain.reshape(1, D)
     (parts,) = call(
         gram_kernel, [state_shape], [HBM] * 2, (keys, values), 4 * tok * D * D, grant=55000,
-        scratch=[pltpu.VMEM(token, BF16), pltpu.VMEM(token, BF16), pltpu.SemaphoreType.DMA((2,))],
+        scratch=[pltpu.VMEM(token, BF16), pltpu.VMEM(token, BF16), pltpu.SemaphoreType.DMA((2, 2))],
     )
     ridge_row = jnp.broadcast_to(ridge.reshape(1, 1), (1, D))
     parts, ridge_row = lax.optimization_barrier((parts, ridge_row))
@@ -320,28 +351,30 @@
         [(token, F32), (token, F32), ((HEADS, 8, D), F32),
          ((chunks, 2 * C, 2 * D), BF16), ((chunks, 3 * C, D), BF16), ((chunks, D, D), F32)],
         [VMEM] * 7,
-        (ridge_row, queries, keys, values, grad_out, gain_row, state),
+        (ridge_row, gain_row, queries, keys, values, grad_out, state),
         10**9,
     )
     sums = exchange(sums, "head")
-    output, grad_q, adjoint, grad_mixed, parts = call(
+    scaled, adjoint, grad_mixed, parts = call(
         adjoint_kernel,
-        [(token, BF16), (token, BF16), (token, F32), (token, F32), state_shape],
+        [(token, BF16), (token, F32), (token, F32), state_shape],
         [VMEM] * 10,
-        (keys, values, grad_out, gain_row, sums, solved, mixed, wide, tall, assoc),
+        (gain_row, keys, values, grad_out, sums, solved, mixed, wide, tall, assoc),
         10**9,
     )
-    local_k, local_v = call(
+    local_k, local_v, output, grad_q = call(
         local_kernel,
-        [(token, F32), (token, F32)],
-        [VMEM] * 5,
-        (keys, values, solved, adjoint, grad_mixed),
+        [(token, F32), (token, F32), (token, BF16), (token, BF16)],
+        [VMEM] * 6,
+        (keys, values, solved, adjoint, grad_mixed, scaled),
         5 * 10**8,
     )
     state = scan_over_seq(after_kernel, parts)
     grad_k, grad_v, grad_gain = call(
         last_kernel, [(token, BF16), (token, BF16), ((1, D), F32)], [VMEM] * 5,
         (keys, values, state, local_k, local_v), 10**8,
+        scratch=[pltpu.VMEM(token, BF16), pltpu.VMEM(token, BF16), pltpu.SemaphoreType.DMA((2, 2))],
+        places=[HBM, HBM, VMEM],
     )
     return output, grad_q, grad_k, grad_v, grad_gain.reshape(D)
 

time: 88.5 us -> 88.7 us (level)
  Pallas kernels: 15.3 us -> 16.2 us
where the time goes in v4:
time: 88.7 us; the launch traced here: 88.3 us
  blocking collectives  57.9 us (65%)
  Pallas kernels  16.2 us (18%)
  waiting for transfers between devices  8.39 us (9%)
  starting transfers between devices  3.86 us (4%)
  between operations  1.33 us (1%)
    all_to_all x4, blocking collectives, exchange(): return lax.all_to_all(array, axis, split_axis=0, concat_axis=0, tiled=True)  57.9 us
    pallas_call x7, Pallas kernels, call(): pl.pallas_call(kernel, out_shape=[jax.ShapeDtypeStruct(s, t) for s, t in...  16.2 us
    all_to_all x1, waiting for transfers between devices, exchange(): return lax.all_to_all(array, axis, split_axis=0, concat_axis=0, tiled=True)  8.39 us
    all_to_all x1, starting transfers between devices, exchange(): return lax.all_to_all(array, axis, split_axis=0, concat_axis=0, tiled=True)  3.86 us
  transfers between devices with their start and end apart: 1, of which 1 were waited for; matrix products, arithmetic and copies ran while one was open for 0% of the time, Pallas kernels for 2%

profile of v4, /device:TPU:8, one launch (start us, length us, event | category | flops | bytes accessed | tf_op | source)
XLA Modules:
  0.0 88.3 jit_solution(363708329160788344)
XLA Ops:
  1.3 1.2 %shard_map.101 = f32[256,128]{1,0:T(8,128)S(1)} custom-call(bf16[512,128]{1,0:T(8,128)(2,1)} %k_ref.7, bf16[512,128]{1,0:T(8,128)(2,1)} %v_ref.7), custom_call_target="tpu_custom_call" | custom-call | flops 33554432 | bytes 262144 | tf_op jit(solution)/shard_map/pallas_call | solution.py:56
  2.5 21.6 %all_to_all.25.a_ref = f32[32,8,128]{2,1,0:T(8,128)S(1)} all-to-all(f32[32,8,128]{2,1,0:T(8,128)S(1)} %bitcast.9), channel_id=1, replica_groups=mesh['z'=8,'x'=4,'head'=8] {'z','x'}, dimensions={0} | all-to-all | bytes 262144 | tf_op jit(solution)/shard_map/all_to_all | solution.py:325
  24.2 0.0 copy-start.2
  24.2 0.0 copy-start.3
  24.2 0.0 copy-start
  24.2 0.0 copy-start.1
  24.2 14.0 %all_to_all.26 = f32[32,8,128]{2,1,0:T(8,128)S(1)} all-to-all(f32[32,8,128]{2,1,0:T(8,128)S(1)} %shard_map.102), channel_id=1, replica_groups=mesh['z'=8,'x'=4,'head'=8] {'z','x'}, dimensions={0} | all-to-all | bytes 262144 | tf_op jit(solution)/shard_map/all_to_all | solution.py:325
  38.2 0.0 copy-start.4
  38.2 0.0 copy-done.2
  38.2 0.0 copy-done.3
  38.2 0.0 copy-done
  38.2 0.0 copy-done.1
  38.2 0.6 copy-done.4
  38.9 5.2 %shard_map.103 = (f32[512,128]{1,0:T(8,128)S(1)}, f32[512,128]{1,0:T(8,128)S(1)}, f32[8,8,128]{2,1,0:T(8,128)S(1)}, bf16[4,256,256]{2,1,0:T(8,128)(2,1)S(1)}, bf...) custom-call(f32[1,128]{1,0:T(1,128)S(1)} %broadcast_in_dim.8.ridge_ref, f32[1,128]{1,0:T(1,128)S(1)} %bitcast.12, ...), custom_call_target="tpu_custom_call" | custom-call | flops 1000000000 | bytes 656384 | tf_op jit(solution)/shard_map/pallas_call | solution.py:56
  44.0 8.7 %all_to_all.27.sums_ref = f32[8,8,128]{2,1,0:T(8,128)S(1)} all-to-all(f32[8,8,128]{2,1,0:T(8,128)S(1)} %get-tuple-element.27), channel_id=1, replica_groups=mesh['z'=8,'x'=4,'head'=8] {'head'}, dimensions={0} | all-to-all | bytes 65536 | tf_op jit(solution)/shard_map/all_to_all | solution.py:325
  52.7 5.3 %shard_map.104 = (bf16[512,128]{1,0:T(8,128)(2,1)S(1)}, f32[512,128]{1,0:T(8,128)S(1)}, f32[512,128]{1,0:T(8,128)S(1)}, f32[256,128]{1,0:T(8,128)S(1)}) custom-call(f32[1,128]{1,0:T(1,128)S(1)} %bitcast.13, bf16[512,128]{1,0:T(8,128)(2,1)S(1)} %copy-done, bf16[512,128]{1,0:T(8,128)(2,1)S(1)} %copy-done.1, bf16[512,128]{1,0:T(8,128)(2,1)S(1)} %copy-done.3, ...), custom_call_target="tpu_custom_call" | custom-call | flops 1000000000 | bytes 2130432 | tf_op jit(solution)/shard_map/pallas_call | solution.py:56
  58.0 13.6 %all_to_all.28.a_ref = f32[32,8,128]{2,1,0:T(8,128)S(1)} all-to-all(f32[32,8,128]{2,1,0:T(8,128)S(1)} %bitcast.10), channel_id=1, replica_groups=mesh['z'=8,'x'=4,'head'=8] {'z','x'}, dimensions={0} | all-to-all | bytes 262144 | tf_op jit(solution)/shard_map/all_to_all | solution.py:325
  71.6 0.7 shard_map.106
  72.3 3.9 %all-to-all-start.4 = ((f32[32,8,128]{2,1,0:T(8,128)}), f32[32,8,128]{2,1,0:T(8,128)S(1)}, u32[]{:S(2)}, u32[]{:S(2)}) async-start(f32[32,8,128]{2,1,0:T(8,128)} %shard_map.106), calls=%async_computation.4 | async-start | bytes 262144 | tf_op jit(solution)/shard_map/all_to_all | solution.py:325
  76.1 2.2 %shard_map.105 = (f32[512,128]{1,0:T(8,128)S(1)}, f32[512,128]{1,0:T(8,128)S(1)}, bf16[512,128]{1,0:T(8,128)(2,1)}, bf16[512,128]{1,0:T(8,128)(2,1)}) custom-call(bf16[512,128]{1,0:T(8,128)(2,1)S(1)} %copy-done, bf16[512,128]{1,0:T(8,128)(2,1)S(1)} %copy-done.1, f32[512,128]{1,0:T(8,128)S(1)} %get-tuple-element.26.solved_ref, ...), custom_call_target="tpu_custom_call" | custom-call | flops 500000000 | bytes 1179648 | tf_op jit(solution)/shard_map/pallas_call | solution.py:56
  78.3 8.4 %all-to-all-done.4 = f32[32,8,128]{2,1,0:T(8,128)S(1)} async-done(((f32[32,8,128]{2,1,0:T(8,128)}), f32[32,8,128]{2,1,0:T(8,128)S(1)}, u32[]{:S(2)}, u32[]{:S(2)}) %all-to-all-start.4) | async-done | bytes 131104 | tf_op jit(solution)/shard_map/all_to_all | solution.py:325
  86.7 1.6 %shard_map.107 = (bf16[512,128]{1,0:T(8,128)(2,1)}, bf16[512,128]{1,0:T(8,128)(2,1)}, f32[1,128]{1,0:T(1,128)}) custom-call(bf16[512,128]{1,0:T(8,128)(2,1)S(1)} %copy-done, bf16[512,128]{1,0:T(8,128)(2,1)S(1)} %copy-done.1, f32[256,128]{1,0:T(8,128)S(1)} %bitcast.8, f32[512,128]{1,0:T(8,128)S(1)} %get-tuple-element.38.local_k_ref, ...), custom_call_target="tpu_custom_call" | custom-call | flops 100000000 | bytes 917504 | tf_op jit(solution)/shard_map/pallas_call | solution.py:56
  (2 shorter events, 0.0 us)
Async XLA Ops:
  24.2 14.1 %copy-start.2 = (bf16[512,128]{1,0:T(8,128)(2,1)S(1)}, bf16[512,128]{1,0:T(8,128)(2,1)}, u32[]{:S(2)}) copy-start(bf16[512,128]{1,0:T(8,128)(2,1)} %q_ref.1) | copy-start | bytes 393220
  24.2 14.1 %copy-start.3 = (bf16[512,128]{1,0:T(8,128)(2,1)S(1)}, bf16[512,128]{1,0:T(8,128)(2,1)}, u32[]{:S(2)}) copy-start(bf16[512,128]{1,0:T(8,128)(2,1)} %g_ref.3) | copy-start | bytes 393220
  24.2 14.0 %copy-start = (bf16[512,128]{1,0:T(8,128)(2,1)S(1)}, bf16[512,128]{1,0:T(8,128)(2,1)}, u32[]{:S(2)}) copy-start(bf16[512,128]{1,0:T(8,128)(2,1)} %k_ref.7) | copy-start | bytes 393220
  24.2 14.0 %copy-start.1 = (bf16[512,128]{1,0:T(8,128)(2,1)S(1)}, bf16[512,128]{1,0:T(8,128)(2,1)}, u32[]{:S(2)}) copy-start(bf16[512,128]{1,0:T(8,128)(2,1)} %v_ref.7) | copy-start | bytes 393220
  38.2 0.7 copy-start.4
  72.3 14.4 %all-to-all-start.4 = ((f32[32,8,128]{2,1,0:T(8,128)}), f32[32,8,128]{2,1,0:T(8,128)S(1)}, u32[]{:S(2)}, u32[]{:S(2)}) async-start(f32[32,8,128]{2,1,0:T(8,128)} %shard_map.106), calls=%async_computation.4 | async-start | bytes 262144 | tf_op jit(solution)/shard_map/all_to_all | solution.py:325

commit v5 on v4

--- a/solution.py
+++ b/solution.py
@@ -51,13 +51,13 @@
     return jnp.sum(x, axis=-1, keepdims=True)
 
 
-def call(kernel, outs, ins, args, flops, grant=8192, scratch=(), places=None):
+def call(kernel, outs, ins, args, flops, grant=8192, scratch=()):
     size = sum(a.size * a.dtype.itemsize for a in args)
     return pl.pallas_call(
         kernel,
         out_shape=[jax.ShapeDtypeStruct(s, t) for s, t in outs],
         in_specs=ins,
-        out_specs=places or [VMEM] * len(outs),
+        out_specs=[VMEM] * len(outs),
         scratch_shapes=list(scratch),
         compiler_params=pltpu.CompilerParams(vmem_limit_bytes=grant * 2**10),
         cost_estimate=pl.CostEstimate(flops=flops, bytes_accessed=size, transcendentals=0),
@@ -72,22 +72,33 @@
     return both[:, C:] + mm(lanes(s_high, s_low, high), tall)
 
 
-def conjugate(rhs, apply_fn):
-    count = len(rhs)
-    each = range(count)
-    sol = [None] * count
+def conjugate(rhs, wide_ref, tall_ref, keep):
+    each = range(len(rhs))
+    sol = [None] * len(rhs)
     res = list(rhs)
     sea = list(rhs)
     now = [row_sum(r * r) for r in res]
+    res_wide = [mm(lanes(*split2(r)), wide_ref[c]) for c, r in enumerate(res)]
+    sea_wide = list(res_wide)
     for step in range(CG_STEPS):
-        image = [apply_fn(c, sea[c]) for c in each]
+        last = step == CG_STEPS - 1
+        image = []
+        for c in each:
+            inner = jnp.where(keep, sea_wide[c][:, :C], 0.0)
+            s_high, s_low = split2(inner)
+            image.append(sea_wide[c][:, C:] + mm(lanes(s_high, s_low, sea[c].astype(BF16)), tall_ref[c]))
+        if not last:
+            image_wide = [mm(lanes(*split2(image[c])), wide_ref[c]) for c in each]
         alpha = [now[c] / (row_sum(sea[c] * image[c]) + EPS) for c in each]
         sol = [alpha[c] * sea[c] if step == 0 else sol[c] + alpha[c] * sea[c] for c in each]
-        if step == CG_STEPS - 1:
+        if last:
             break
         res = [res[c] - alpha[c] * image[c] for c in each]
         new = [row_sum(res[c] * res[c]) for c in each]
-        sea = [res[c] + new[c] / (now[c] + EPS) * sea[c] for c in each]
+        beta = [new[c] / (now[c] + EPS) for c in each]
+        sea = [res[c] + beta[c] * sea[c] for c in each]
+        res_wide = [res_wide[c] - alpha[c] * image_wide[c] for c in each]
+        sea_wide = [res_wide[c] + beta[c] * sea_wide[c] for c in each]
         now = new
     return sol
 
@@ -171,8 +182,7 @@
             gram = gram + more[:C]
             assoc = assoc + more[C:]
     solved = conjugate(
-        [q_ref[at[c]].astype(F32) for c in each],
-        lambda c, p: masked_apply(p, wide_ref[c], tall_ref[c], keep),
+        [q_ref[at[c]].astype(F32) for c in each], wide_ref, tall_ref, keep
     )
     gain = gain_ref[...]
     ones = jnp.ones((8, 2 * D), BF16)
@@ -230,7 +240,7 @@
         turned.append(lanes(high, low, high))
     part_ref[D + 72 : D + 80] = gain_part
     part_ref[D + 80 :] = jnp.zeros((D - 80, D), F32)
-    adjoint = conjugate(rhs, lambda c, p: masked_apply(p, wide_ref[c], tall_ref[c], keep))
+    adjoint = conjugate(rhs, wide_ref, tall_ref, keep)
     total = None
     for c in each:
         adjoint_ref[at[c]] = adjoint[c]
@@ -286,39 +296,18 @@
             pairs = pair if pairs is None else pairs + pair
 
 
-def key_weights(suffix, pairs):
-    return rows(*split2(suffix), *split2(-pairs))
-
-
 def finish(k, v, suffix, pairs):
     t_high, t_low = split2(suffix.T)
-    return mm(lanes(v, v, k, k), key_weights(suffix, pairs)), mm(lanes(k, k), rows(t_high, t_low))
-
-
-def last_kernel(k_ref, v_ref, state_ref, local_k_ref, local_v_ref, grad_k_hbm, grad_v_hbm, gain_ref,
-                grad_k_ref, grad_v_ref, sem):
-    suffix = state_ref[:D]
+    weights = rows(*split2(suffix), *split2(-pairs))
+    return mm(lanes(v, v, k, k), weights), mm(lanes(k, k), rows(t_high, t_low))
+
+
+def last_kernel(k_ref, v_ref, state_ref, local_k_ref, local_v_ref, grad_k_ref, grad_v_ref, gain_ref):
     pairs = unpack(state_ref[D : D + 64], state_ref[D + 64 : D + 65])
-    half = k_ref.shape[0] // 2
-    copies = []
-    t_high, t_low = split2(suffix.T)
-    turned = rows(t_high, t_low)
-    direct = key_weights(suffix, pairs)
-    for n in range(2):
-        at = pl.ds(half * n, half)
-        k = k_ref[at]
-        grad_v_ref[at] = (local_v_ref[at] + mm(lanes(k, k), turned)).astype(BF16)
-        copies.append(pltpu.make_async_copy(grad_v_ref.at[at], grad_v_hbm.at[at], sem.at[n, 0]))
-        copies[-1].start()
-    for n in range(2):
-        at = pl.ds(half * n, half)
-        k, v = k_ref[at], v_ref[at]
-        grad_k_ref[at] = (local_k_ref[at] + mm(lanes(v, v, k, k), direct)).astype(BF16)
-        copies.append(pltpu.make_async_copy(grad_k_ref.at[at], grad_k_hbm.at[at], sem.at[n, 1]))
-        copies[-1].start()
+    grad_k, grad_v = finish(k_ref[...], v_ref[...], state_ref[:D], pairs)
+    grad_v_ref[...] = (local_v_ref[...] + grad_v).astype(BF16)
+    grad_k_ref[...] = (local_k_ref[...] + grad_k).astype(BF16)
     gain_ref[...] = jnp.sum(state_ref[D + 72 : D + 80], axis=0, keepdims=True)
-    for copy in copies:
-        copy.wait()
 
 
 def exchange(array, axis):
@@ -354,7 +343,7 @@
         (ridge_row, gain_row, queries, keys, values, grad_out, state),
         10**9,
     )
-    sums = exchange(sums, "head")
+    sums = exchange(sums, ("core", "y"))
     scaled, adjoint, grad_mixed, parts = call(
         adjoint_kernel,
         [(token, BF16), (token, F32), (token, F32), state_shape],
@@ -373,19 +362,18 @@
     grad_k, grad_v, grad_gain = call(
         last_kernel, [(token, BF16), (token, BF16), ((1, D), F32)], [VMEM] * 5,
         (keys, values, state, local_k, local_v), 10**8,
-        scratch=[pltpu.VMEM(token, BF16), pltpu.VMEM(token, BF16), pltpu.SemaphoreType.DMA((2, 2))],
-        places=[HBM, HBM, VMEM],
     )
     return output, grad_q, grad_k, grad_v, grad_gain.reshape(D)
 
 
 def solution(mesh):
-    split = Mesh(mesh.devices.reshape(ZN, XN, mesh.shape["head"]), ("z", "x", "head"))
-    tokens = P(SEQ, "head")
+    split = Mesh(mesh.devices.reshape(ZN, XN, mesh.shape["head"] // 2, 2), ("z", "x", "y", "core"))
+    head = ("y", "core")
+    tokens = P(SEQ, head)
     return jax.shard_map(
         per_device,
         mesh=split,
-        in_specs=(tokens, tokens, tokens, P("head"), P("head"), tokens),
-        out_specs=(tokens, tokens, tokens, tokens, P("head")),
+        in_specs=(tokens, tokens, tokens, P(head), P(head), tokens),
+        out_specs=(tokens, tokens, tokens, tokens, P(head)),
         check_vma=False,
     )

time: 88.7 us -> 85.7 us (0.966)
  Pallas kernels: 16.2 us -> 12.8 us
    pallas_call x7, Pallas kernels: 16.2 us -> 12.8 us  [call(): pl.pallas_call(kernel, out_shape=[jax.ShapeDtypeStruct(s, t) for s, t in...]
  transfers between devices with their start and end apart: 1 -> 1, of which waited for: 1 -> 1; matrix products, arithmetic and copies ran while one was open for 0% -> 0% of each run, Pallas kernels for 2% -> 3%
where the time goes in v5:
time: 85.7 us; the launch traced here: 85.4 us
  blocking collectives  58.4 us (68%)
  Pallas kernels  12.8 us (15%)
  waiting for transfers between devices  8.4 us (10%)
  starting transfers between devices  3.86 us (5%)
  between operations  1.33 us (2%)
    all_to_all x4, blocking collectives, exchange(): return lax.all_to_all(array, axis, split_axis=0, concat_axis=0, tiled=True)  58.4 us
    pallas_call x7, Pallas kernels, call(): pl.pallas_call(kernel, out_shape=[jax.ShapeDtypeStruct(s, t) for s, t in...  12.8 us
    all_to_all x1, waiting for transfers between devices, exchange(): return lax.all_to_all(array, axis, split_axis=0, concat_axis=0, tiled=True)  8.4 us
    all_to_all x1, starting transfers between devices, exchange(): return lax.all_to_all(array, axis, split_axis=0, concat_axis=0, tiled=True)  3.86 us
  transfers between devices with their start and end apart: 1, of which 1 were waited for; matrix products, arithmetic and copies ran while one was open for 0% of the time, Pallas kernels for 3%

profile of v5, /device:TPU:8, one launch (start us, length us, event | category | flops | bytes accessed | tf_op | source)
XLA Modules:
  0.0 85.4 jit_solution(2746752003229474)
XLA Ops:
  1.3 1.2 %shard_map.101 = f32[256,128]{1,0:T(8,128)S(1)} custom-call(bf16[512,128]{1,0:T(8,128)(2,1)} %k_ref.7, bf16[512,128]{1,0:T(8,128)(2,1)} %v_ref.7), custom_call_target="tpu_custom_call" | custom-call | flops 33554432 | bytes 262144 | tf_op jit(solution)/shard_map/pallas_call | solution.py:56
  2.5 21.6 %all_to_all.25.a_ref = f32[32,8,128]{2,1,0:T(8,128)S(1)} all-to-all(f32[32,8,128]{2,1,0:T(8,128)S(1)} %bitcast.9), channel_id=1, replica_groups=mesh['z'=8,'x'=4,'y'=4,'core'=2] {'z','x'}, dimensions={0} | all-to-all | bytes 262144 | tf_op jit(solution)/shard_map/all_to_all | solution.py:314
  24.2 0.0 copy-start.2
  24.2 0.0 copy-start.3
  24.2 0.0 copy-start
  24.2 0.0 copy-start.1
  24.2 14.0 %all_to_all.26 = f32[32,8,128]{2,1,0:T(8,128)S(1)} all-to-all(f32[32,8,128]{2,1,0:T(8,128)S(1)} %shard_map.102), channel_id=1, replica_groups=mesh['z'=8,'x'=4,'y'=4,'core'=2] {'z','x'}, dimensions={0} | all-to-all | bytes 262144 | tf_op jit(solution)/shard_map/all_to_all | solution.py:314
  38.2 0.0 copy-start.4
  38.2 0.0 copy-done.2
  38.2 0.0 copy-done.3
  38.2 0.0 copy-done
  38.2 0.0 copy-done.1
  38.2 0.6 copy-done.4
  38.9 3.8 %shard_map.103 = (f32[512,128]{1,0:T(8,128)S(1)}, f32[512,128]{1,0:T(8,128)S(1)}, f32[8,8,128]{2,1,0:T(8,128)S(1)}, bf16[4,256,256]{2,1,0:T(8,128)(2,1)S(1)}, bf...) custom-call(f32[1,128]{1,0:T(1,128)S(1)} %broadcast_in_dim.8.ridge_ref, f32[1,128]{1,0:T(1,128)S(1)} %bitcast.12, ...), custom_call_target="tpu_custom_call" | custom-call | flops 1000000000 | bytes 656384 | tf_op jit(solution)/shard_map/pallas_call | solution.py:56
  42.7 8.7 %all_to_all.27.sums_ref = f32[8,8,128]{2,1,0:T(8,128)S(1)} all-to-all(f32[8,8,128]{2,1,0:T(8,128)S(1)} %get-tuple-element.27), channel_id=1, replica_groups=mesh['z'=8,'x'=4,'y'=4,'core'=2] {'core','y'}, dimensions={0} | all-to-all | bytes 65536 | tf_op jit(solution)/shard_map/all_to_all | solution.py:314
  51.3 3.7 %shard_map.104 = (bf16[512,128]{1,0:T(8,128)(2,1)S(1)}, f32[512,128]{1,0:T(8,128)S(1)}, f32[512,128]{1,0:T(8,128)S(1)}, f32[256,128]{1,0:T(8,128)S(1)}) custom-call(f32[1,128]{1,0:T(1,128)S(1)} %bitcast.13, bf16[512,128]{1,0:T(8,128)(2,1)S(1)} %copy-done, bf16[512,128]{1,0:T(8,128)(2,1)S(1)} %copy-done.1, bf16[512,128]{1,0:T(8,128)(2,1)S(1)} %copy-done.3, ...), custom_call_target="tpu_custom_call" | custom-call | flops 1000000000 | bytes 2130432 | tf_op jit(solution)/shard_map/pallas_call | solution.py:56
  55.1 14.1 %all_to_all.28.a_ref = f32[32,8,128]{2,1,0:T(8,128)S(1)} all-to-all(f32[32,8,128]{2,1,0:T(8,128)S(1)} %bitcast.10), channel_id=1, replica_groups=mesh['z'=8,'x'=4,'y'=4,'core'=2] {'z','x'}, dimensions={0} | all-to-all | bytes 262144 | tf_op jit(solution)/shard_map/all_to_all | solution.py:314
  69.1 0.7 shard_map.106
  69.8 3.9 %all-to-all-start.4 = ((f32[32,8,128]{2,1,0:T(8,128)}), f32[32,8,128]{2,1,0:T(8,128)S(1)}, u32[]{:S(2)}, u32[]{:S(2)}) async-start(f32[32,8,128]{2,1,0:T(8,128)} %shard_map.106), calls=%async_computation.4 | async-start | bytes 262144 | tf_op jit(solution)/shard_map/all_to_all | solution.py:314
  73.7 2.2 %shard_map.105 = (f32[512,128]{1,0:T(8,128)S(1)}, f32[512,128]{1,0:T(8,128)S(1)}, bf16[512,128]{1,0:T(8,128)(2,1)}, bf16[512,128]{1,0:T(8,128)(2,1)}) custom-call(bf16[512,128]{1,0:T(8,128)(2,1)S(1)} %copy-done, bf16[512,128]{1,0:T(8,128)(2,1)S(1)} %copy-done.1, f32[512,128]{1,0:T(8,128)S(1)} %get-tuple-element.26.solved_ref, ...), custom_call_target="tpu_custom_call" | custom-call | flops 500000000 | bytes 1179648 | tf_op jit(solution)/shard_map/pallas_call | solution.py:56
  75.9 8.4 %all-to-all-done.4 = f32[32,8,128]{2,1,0:T(8,128)S(1)} async-done(((f32[32,8,128]{2,1,0:T(8,128)}), f32[32,8,128]{2,1,0:T(8,128)S(1)}, u32[]{:S(2)}, u32[]{:S(2)}) %all-to-all-start.4) | async-done | bytes 131104 | tf_op jit(solution)/shard_map/all_to_all | solution.py:314
  84.2 1.1 %shard_map.107 = (bf16[512,128]{1,0:T(8,128)(2,1)}, bf16[512,128]{1,0:T(8,128)(2,1)}, f32[1,128]{1,0:T(1,128)}) custom-call(bf16[512,128]{1,0:T(8,128)(2,1)S(1)} %copy-done, bf16[512,128]{1,0:T(8,128)(2,1)S(1)} %copy-done.1, f32[256,128]{1,0:T(8,128)S(1)} %bitcast.8, f32[512,128]{1,0:T(8,128)S(1)} %get-tuple-element.38.local_k_ref, ...), custom_call_target="tpu_custom_call" | custom-call | flops 100000000 | bytes 917504 | tf_op jit(solution)/shard_map/pallas_call | solution.py:56
  (2 shorter events, 0.0 us)
Async XLA Ops:
  24.2 14.1 %copy-start.2 = (bf16[512,128]{1,0:T(8,128)(2,1)S(1)}, bf16[512,128]{1,0:T(8,128)(2,1)}, u32[]{:S(2)}) copy-start(bf16[512,128]{1,0:T(8,128)(2,1)} %q_ref.1) | copy-start | bytes 393220
  24.2 14.1 %copy-start.3 = (bf16[512,128]{1,0:T(8,128)(2,1)S(1)}, bf16[512,128]{1,0:T(8,128)(2,1)}, u32[]{:S(2)}) copy-start(bf16[512,128]{1,0:T(8,128)(2,1)} %g_ref.3) | copy-start | bytes 393220
  24.2 14.0 %copy-start = (bf16[512,128]{1,0:T(8,128)(2,1)S(1)}, bf16[512,128]{1,0:T(8,128)(2,1)}, u32[]{:S(2)}) copy-start(bf16[512,128]{1,0:T(8,128)(2,1)} %k_ref.7) | copy-start | bytes 393220
  24.2 14.0 %copy-start.1 = (bf16[512,128]{1,0:T(8,128)(2,1)S(1)}, bf16[512,128]{1,0:T(8,128)(2,1)}, u32[]{:S(2)}) copy-start(bf16[512,128]{1,0:T(8,128)(2,1)} %v_ref.7) | copy-start | bytes 393220
  38.2 0.7 copy-start.4
  69.8 14.4 %all-to-all-start.4 = ((f32[32,8,128]{2,1,0:T(8,128)}), f32[32,8,128]{2,1,0:T(8,128)S(1)}, u32[]{:S(2)}, u32[]{:S(2)}) async-start(f32[32,8,128]{2,1,0:T(8,128)} %shard_map.106), calls=%async_computation.4 | async-start | bytes 262144 | tf_op jit(solution)/shard_map/all_to_all | solution.py:314

commit v6 on v5

--- a/solution.py
+++ b/solution.py
@@ -72,7 +72,7 @@
     return both[:, C:] + mm(lanes(s_high, s_low, high), tall)
 
 
-def conjugate(rhs, wide_ref, tall_ref, keep):
+def conjugate(rhs, wide_ref, tall_ref, keep, with_inner=False):
     each = range(len(rhs))
     sol = [None] * len(rhs)
     res = list(rhs)
@@ -80,6 +80,7 @@
     now = [row_sum(r * r) for r in res]
     res_wide = [mm(lanes(*split2(r)), wide_ref[c]) for c, r in enumerate(res)]
     sea_wide = list(res_wide)
+    sol_inner = [None] * len(rhs)
     for step in range(CG_STEPS):
         last = step == CG_STEPS - 1
         image = []
@@ -91,6 +92,9 @@
             image_wide = [mm(lanes(*split2(image[c])), wide_ref[c]) for c in each]
         alpha = [now[c] / (row_sum(sea[c] * image[c]) + EPS) for c in each]
         sol = [alpha[c] * sea[c] if step == 0 else sol[c] + alpha[c] * sea[c] for c in each]
+        if with_inner:
+            inner = [alpha[c] * sea_wide[c][:, :C] for c in each]
+            sol_inner = inner if step == 0 else [sol_inner[c] + inner[c] for c in each]
         if last:
             break
         res = [res[c] - alpha[c] * image[c] for c in each]
@@ -100,7 +104,7 @@
         res_wide = [res_wide[c] - alpha[c] * image_wide[c] for c in each]
         sea_wide = [res_wide[c] + beta[c] * sea_wide[c] for c in each]
         now = new
-    return sol
+    return sol, sol_inner
 
 
 def gram_kernel(k_hbm, v_hbm, out_ref, k_ref, v_ref, sem):
@@ -165,12 +169,10 @@
     eye = iota2(0) == iota2(1)
     gram = state_ref[:D] + jnp.where(eye, ridge_ref[...], 0.0)
     assoc = state_ref[D:]
-    turned = []
     for c in each:
         k = k_ref[at[c]]
         v = v_ref[at[c]]
         k_t = k.T
-        turned.append(k_t)
         high, low = split2(gram)
         top = lanes(k_t, high)
         wide_ref[c, :C] = top
@@ -181,16 +183,20 @@
             more = mm(rows(k_t, v.T), k)
             gram = gram + more[:C]
             assoc = assoc + more[C:]
-    solved = conjugate(
-        [q_ref[at[c]].astype(F32) for c in each], wide_ref, tall_ref, keep
+    weights = []
+    for c in each:
+        v = v_ref[at[c]]
+        high, low = split2(assoc_ref[c].T)
+        weights.append(rows(v, v, high, high, low))
+    solved, inner = conjugate(
+        [q_ref[at[c]].astype(F32) for c in each], wide_ref, tall_ref, keep, True
     )
     gain = gain_ref[...]
     ones = jnp.ones((8, 2 * D), BF16)
     for c in each:
-        high, low = split2(assoc_ref[c].T)
-        top = lanes(turned[c], high)
-        v = v_ref[at[c]]
-        mixed = masked_apply(solved[c], rows(top, top), rows(v, v, low), keep)
+        x_high, x_low = split2(solved[c])
+        s_high, s_low = split2(jnp.where(keep, inner[c], 0.0))
+        mixed = mm(lanes(s_high, s_low, x_high, x_low, x_high), weights[c])
         solved_ref[at[c]] = solved[c]
         mixed_ref[at[c]] = mixed
         square = mixed * mixed
@@ -240,7 +246,7 @@
         turned.append(lanes(high, low, high))
     part_ref[D + 72 : D + 80] = gain_part
     part_ref[D + 80 :] = jnp.zeros((D - 80, D), F32)
-    adjoint = conjugate(rhs, wide_ref, tall_ref, keep)
+    adjoint, _ = conjugate(rhs, wide_ref, tall_ref, keep)
     total = None
     for c in each:
         adjoint_ref[at[c]] = adjoint[c]

time: 85.7 us -> 85.5 us (level)
  no operation moved by 1% of the time
where the time goes in v6:
time: 85.5 us; the launch traced here: 85.1 us
  blocking collectives  58.4 us (68%)
  Pallas kernels  12.5 us (15%)
  waiting for transfers between devices  8.46 us (10%)
  starting transfers between devices  3.86 us (5%)
  between operations  1.33 us (2%)
    all_to_all x4, blocking collectives, exchange(): return lax.all_to_all(array, axis, split_axis=0, concat_axis=0, tiled=True)  58.4 us
    pallas_call x7, Pallas kernels, call(): pl.pallas_call(kernel, out_shape=[jax.ShapeDtypeStruct(s, t) for s, t in...  12.5 us
    all_to_all x1, waiting for transfers between devices, exchange(): return lax.all_to_all(array, axis, split_axis=0, concat_axis=0, tiled=True)  8.46 us
    all_to_all x1, starting transfers between devices, exchange(): return lax.all_to_all(array, axis, split_axis=0, concat_axis=0, tiled=True)  3.86 us
  transfers between devices with their start and end apart: 1, of which 1 were waited for; matrix products, arithmetic and copies ran while one was open for 0% of the time, Pallas kernels for 3%

profile of v6, /device:TPU:8, one launch (start us, length us, event | category | flops | bytes accessed | tf_op | source)
XLA Modules:
  0.0 85.1 jit_solution(10056898058881851723)
XLA Ops:
  1.3 1.2 %shard_map.101 = f32[256,128]{1,0:T(8,128)S(1)} custom-call(bf16[512,128]{1,0:T(8,128)(2,1)} %k_ref.7, bf16[512,128]{1,0:T(8,128)(2,1)} %v_ref.7), custom_call_target="tpu_custom_call" | custom-call | flops 33554432 | bytes 262144 | tf_op jit(solution)/shard_map/pallas_call | solution.py:56
  2.5 21.6 %all_to_all.25.a_ref = f32[32,8,128]{2,1,0:T(8,128)S(1)} all-to-all(f32[32,8,128]{2,1,0:T(8,128)S(1)} %bitcast.9), channel_id=1, replica_groups=mesh['z'=8,'x'=4,'y'=4,'core'=2] {'z','x'}, dimensions={0} | all-to-all | bytes 262144 | tf_op jit(solution)/shard_map/all_to_all | solution.py:320
  24.2 0.0 copy-start.2
  24.2 0.0 copy-start.3
  24.2 0.0 copy-start
  24.2 0.0 copy-start.1
  24.2 14.0 %all_to_all.26 = f32[32,8,128]{2,1,0:T(8,128)S(1)} all-to-all(f32[32,8,128]{2,1,0:T(8,128)S(1)} %shard_map.102), channel_id=1, replica_groups=mesh['z'=8,'x'=4,'y'=4,'core'=2] {'z','x'}, dimensions={0} | all-to-all | bytes 262144 | tf_op jit(solution)/shard_map/all_to_all | solution.py:320
  38.2 0.0 copy-start.4
  38.2 0.0 copy-done.2
  38.2 0.0 copy-done.3
  38.2 0.0 copy-done
  38.2 0.0 copy-done.1
  38.2 0.6 copy-done.4
  38.9 3.5 %shard_map.103 = (f32[512,128]{1,0:T(8,128)S(1)}, f32[512,128]{1,0:T(8,128)S(1)}, f32[8,8,128]{2,1,0:T(8,128)S(1)}, bf16[4,256,256]{2,1,0:T(8,128)(2,1)S(1)}, bf...) custom-call(f32[1,128]{1,0:T(1,128)S(1)} %broadcast_in_dim.8.ridge_ref, f32[1,128]{1,0:T(1,128)S(1)} %bitcast.12, ...), custom_call_target="tpu_custom_call" | custom-call | flops 1000000000 | bytes 656384 | tf_op jit(solution)/shard_map/pallas_call | solution.py:56
  42.3 8.7 %all_to_all.27.sums_ref = f32[8,8,128]{2,1,0:T(8,128)S(1)} all-to-all(f32[8,8,128]{2,1,0:T(8,128)S(1)} %get-tuple-element.27), channel_id=1, replica_groups=mesh['z'=8,'x'=4,'y'=4,'core'=2] {'core','y'}, dimensions={0} | all-to-all | bytes 65536 | tf_op jit(solution)/shard_map/all_to_all | solution.py:320
  51.0 3.7 %shard_map.104 = (bf16[512,128]{1,0:T(8,128)(2,1)S(1)}, f32[512,128]{1,0:T(8,128)S(1)}, f32[512,128]{1,0:T(8,128)S(1)}, f32[256,128]{1,0:T(8,128)S(1)}) custom-call(f32[1,128]{1,0:T(1,128)S(1)} %bitcast.13, bf16[512,128]{1,0:T(8,128)(2,1)S(1)} %copy-done, bf16[512,128]{1,0:T(8,128)(2,1)S(1)} %copy-done.1, bf16[512,128]{1,0:T(8,128)(2,1)S(1)} %copy-done.3, ...), custom_call_target="tpu_custom_call" | custom-call | flops 1000000000 | bytes 2130432 | tf_op jit(solution)/shard_map/pallas_call | solution.py:56
  54.7 14.1 %all_to_all.28.a_ref = f32[32,8,128]{2,1,0:T(8,128)S(1)} all-to-all(f32[32,8,128]{2,1,0:T(8,128)S(1)} %bitcast.10), channel_id=1, replica_groups=mesh['z'=8,'x'=4,'y'=4,'core'=2] {'z','x'}, dimensions={0} | all-to-all | bytes 262144 | tf_op jit(solution)/shard_map/all_to_all | solution.py:320
  68.8 0.7 shard_map.106
  69.5 3.9 %all-to-all-start.4 = ((f32[32,8,128]{2,1,0:T(8,128)}), f32[32,8,128]{2,1,0:T(8,128)S(1)}, u32[]{:S(2)}, u32[]{:S(2)}) async-start(f32[32,8,128]{2,1,0:T(8,128)} %shard_map.106), calls=%async_computation.4 | async-start | bytes 262144 | tf_op jit(solution)/shard_map/all_to_all | solution.py:320
  73.4 2.2 %shard_map.105 = (f32[512,128]{1,0:T(8,128)S(1)}, f32[512,128]{1,0:T(8,128)S(1)}, bf16[512,128]{1,0:T(8,128)(2,1)}, bf16[512,128]{1,0:T(8,128)(2,1)}) custom-call(bf16[512,128]{1,0:T(8,128)(2,1)S(1)} %copy-done, bf16[512,128]{1,0:T(8,128)(2,1)S(1)} %copy-done.1, f32[512,128]{1,0:T(8,128)S(1)} %get-tuple-element.26.solved_ref, ...), custom_call_target="tpu_custom_call" | custom-call | flops 500000000 | bytes 1179648 | tf_op jit(solution)/shard_map/pallas_call | solution.py:56
  75.5 8.5 %all-to-all-done.4 = f32[32,8,128]{2,1,0:T(8,128)S(1)} async-done(((f32[32,8,128]{2,1,0:T(8,128)}), f32[32,8,128]{2,1,0:T(8,128)S(1)}, u32[]{:S(2)}, u32[]{:S(2)}) %all-to-all-start.4) | async-done | bytes 131104 | tf_op jit(solution)/shard_map/all_to_all | solution.py:320
  84.0 1.1 %shard_map.107 = (bf16[512,128]{1,0:T(8,128)(2,1)}, bf16[512,128]{1,0:T(8,128)(2,1)}, f32[1,128]{1,0:T(1,128)}) custom-call(bf16[512,128]{1,0:T(8,128)(2,1)S(1)} %copy-done, bf16[512,128]{1,0:T(8,128)(2,1)S(1)} %copy-done.1, f32[256,128]{1,0:T(8,128)S(1)} %bitcast.8, f32[512,128]{1,0:T(8,128)S(1)} %get-tuple-element.38.local_k_ref, ...), custom_call_target="tpu_custom_call" | custom-call | flops 100000000 | bytes 917504 | tf_op jit(solution)/shard_map/pallas_call | solution.py:56
  (2 shorter events, 0.0 us)
Async XLA Ops:
  24.2 14.1 %copy-start.2 = (bf16[512,128]{1,0:T(8,128)(2,1)S(1)}, bf16[512,128]{1,0:T(8,128)(2,1)}, u32[]{:S(2)}) copy-start(bf16[512,128]{1,0:T(8,128)(2,1)} %q_ref.1) | copy-start | bytes 393220
  24.2 14.1 %copy-start.3 = (bf16[512,128]{1,0:T(8,128)(2,1)S(1)}, bf16[512,128]{1,0:T(8,128)(2,1)}, u32[]{:S(2)}) copy-start(bf16[512,128]{1,0:T(8,128)(2,1)} %g_ref.3) | copy-start | bytes 393220
  24.2 14.0 %copy-start = (bf16[512,128]{1,0:T(8,128)(2,1)S(1)}, bf16[512,128]{1,0:T(8,128)(2,1)}, u32[]{:S(2)}) copy-start(bf16[512,128]{1,0:T(8,128)(2,1)} %k_ref.7) | copy-start | bytes 393220
  24.2 14.0 %copy-start.1 = (bf16[512,128]{1,0:T(8,128)(2,1)S(1)}, bf16[512,128]{1,0:T(8,128)(2,1)}, u32[]{:S(2)}) copy-start(bf16[512,128]{1,0:T(8,128)(2,1)} %v_ref.7) | copy-start | bytes 393220
  38.2 0.7 copy-start.4
  69.5 14.5 %all-to-all-start.4 = ((f32[32,8,128]{2,1,0:T(8,128)}), f32[32,8,128]{2,1,0:T(8,128)S(1)}, u32[]{:S(2)}, u32[]{:S(2)}) async-start(f32[32,8,128]{2,1,0:T(8,128)} %shard_map.106), calls=%async_computation.4 | async-start | bytes 262144 | tf_op jit(solution)/shard_map/all_to_all | solution.py:320

commit v7 on v6

--- a/solution.py
+++ b/solution.py
@@ -72,13 +72,16 @@
     return both[:, C:] + mm(lanes(s_high, s_low, high), tall)
 
 
-def conjugate(rhs, wide_ref, tall_ref, keep, with_inner=False):
+def conjugate(rhs, wide_ref, tall_ref, keep, exact=None, with_inner=False):
     each = range(len(rhs))
     sol = [None] * len(rhs)
     res = list(rhs)
     sea = list(rhs)
     now = [row_sum(r * r) for r in res]
-    res_wide = [mm(lanes(*split2(r)), wide_ref[c]) for c, r in enumerate(res)]
+    if exact is None:
+        res_wide = [mm(lanes(*split2(r)), wide_ref[c]) for c, r in enumerate(res)]
+    else:
+        res_wide = [mm(r, wide_ref[c, :C]) for c, r in enumerate(exact)]
     sea_wide = list(res_wide)
     sol_inner = [None] * len(rhs)
     for step in range(CG_STEPS):
@@ -189,7 +192,7 @@
         high, low = split2(assoc_ref[c].T)
         weights.append(rows(v, v, high, high, low))
     solved, inner = conjugate(
-        [q_ref[at[c]].astype(F32) for c in each], wide_ref, tall_ref, keep, True
+        [q_ref[at[c]].astype(F32) for c in each], wide_ref, tall_ref, keep, [q_ref[at[c]] for c in each], True
     )
     gain = gain_ref[...]
     ones = jnp.ones((8, 2 * D), BF16)

time: 85.5 us -> 85.5 us (level)
  no operation moved by 1% of the time
where the time goes in v7:
time: 85.5 us; the launch traced here: 85.1 us
  blocking collectives  58.4 us (68%)
  Pallas kernels  12.4 us (15%)
  waiting for transfers between devices  8.46 us (10%)
  starting transfers between devices  3.86 us (5%)
  between operations  1.33 us (2%)
    all_to_all x4, blocking collectives, exchange(): return lax.all_to_all(array, axis, split_axis=0, concat_axis=0, tiled=True)  58.4 us
    pallas_call x7, Pallas kernels, call(): pl.pallas_call(kernel, out_shape=[jax.ShapeDtypeStruct(s, t) for s, t in...  12.4 us
    all_to_all x1, waiting for transfers between devices, exchange(): return lax.all_to_all(array, axis, split_axis=0, concat_axis=0, tiled=True)  8.46 us
    all_to_all x1, starting transfers between devices, exchange(): return lax.all_to_all(array, axis, split_axis=0, concat_axis=0, tiled=True)  3.86 us
  transfers between devices with their start and end apart: 1, of which 1 were waited for; matrix products, arithmetic and copies ran while one was open for 0% of the time, Pallas kernels for 3%

profile of v7, /device:TPU:8, one launch (start us, length us, event | category | flops | bytes accessed | tf_op | source)
XLA Modules:
  0.0 85.1 jit_solution(8530321241150443560)
XLA Ops:
  1.3 1.2 %shard_map.101 = f32[256,128]{1,0:T(8,128)S(1)} custom-call(bf16[512,128]{1,0:T(8,128)(2,1)} %k_ref.7, bf16[512,128]{1,0:T(8,128)(2,1)} %v_ref.7), custom_call_target="tpu_custom_call" | custom-call | flops 33554432 | bytes 262144 | tf_op jit(solution)/shard_map/pallas_call | solution.py:56
  2.5 21.6 %all_to_all.25.a_ref = f32[32,8,128]{2,1,0:T(8,128)S(1)} all-to-all(f32[32,8,128]{2,1,0:T(8,128)S(1)} %bitcast.9), channel_id=1, replica_groups=mesh['z'=8,'x'=4,'y'=4,'core'=2] {'z','x'}, dimensions={0} | all-to-all | bytes 262144 | tf_op jit(solution)/shard_map/all_to_all | solution.py:323
  24.2 0.0 copy-start.2
  24.2 0.0 copy-start.3
  24.2 0.0 copy-start
  24.2 0.0 copy-start.1
  24.2 14.0 %all_to_all.26 = f32[32,8,128]{2,1,0:T(8,128)S(1)} all-to-all(f32[32,8,128]{2,1,0:T(8,128)S(1)} %shard_map.102), channel_id=1, replica_groups=mesh['z'=8,'x'=4,'y'=4,'core'=2] {'z','x'}, dimensions={0} | all-to-all | bytes 262144 | tf_op jit(solution)/shard_map/all_to_all | solution.py:323
  38.2 0.0 copy-start.4
  38.2 0.0 copy-done.2
  38.2 0.0 copy-done.3
  38.2 0.0 copy-done
  38.2 0.0 copy-done.1
  38.2 0.6 copy-done.4
  38.9 3.5 %shard_map.103 = (f32[512,128]{1,0:T(8,128)S(1)}, f32[512,128]{1,0:T(8,128)S(1)}, f32[8,8,128]{2,1,0:T(8,128)S(1)}, bf16[4,256,256]{2,1,0:T(8,128)(2,1)S(1)}, bf...) custom-call(f32[1,128]{1,0:T(1,128)S(1)} %broadcast_in_dim.8.ridge_ref, f32[1,128]{1,0:T(1,128)S(1)} %bitcast.12, ...), custom_call_target="tpu_custom_call" | custom-call | flops 1000000000 | bytes 656384 | tf_op jit(solution)/shard_map/pallas_call | solution.py:56
  42.3 8.7 %all_to_all.27.sums_ref = f32[8,8,128]{2,1,0:T(8,128)S(1)} all-to-all(f32[8,8,128]{2,1,0:T(8,128)S(1)} %get-tuple-element.27), channel_id=1, replica_groups=mesh['z'=8,'x'=4,'y'=4,'core'=2] {'core','y'}, dimensions={0} | all-to-all | bytes 65536 | tf_op jit(solution)/shard_map/all_to_all | solution.py:323
  51.0 3.7 %shard_map.104 = (bf16[512,128]{1,0:T(8,128)(2,1)S(1)}, f32[512,128]{1,0:T(8,128)S(1)}, f32[512,128]{1,0:T(8,128)S(1)}, f32[256,128]{1,0:T(8,128)S(1)}) custom-call(f32[1,128]{1,0:T(1,128)S(1)} %bitcast.13, bf16[512,128]{1,0:T(8,128)(2,1)S(1)} %copy-done, bf16[512,128]{1,0:T(8,128)(2,1)S(1)} %copy-done.1, bf16[512,128]{1,0:T(8,128)(2,1)S(1)} %copy-done.3, ...), custom_call_target="tpu_custom_call" | custom-call | flops 1000000000 | bytes 2130432 | tf_op jit(solution)/shard_map/pallas_call | solution.py:56
  54.7 14.1 %all_to_all.28.a_ref = f32[32,8,128]{2,1,0:T(8,128)S(1)} all-to-all(f32[32,8,128]{2,1,0:T(8,128)S(1)} %bitcast.10), channel_id=1, replica_groups=mesh['z'=8,'x'=4,'y'=4,'core'=2] {'z','x'}, dimensions={0} | all-to-all | bytes 262144 | tf_op jit(solution)/shard_map/all_to_all | solution.py:323
  68.8 0.7 shard_map.106
  69.5 3.9 %all-to-all-start.4 = ((f32[32,8,128]{2,1,0:T(8,128)}), f32[32,8,128]{2,1,0:T(8,128)S(1)}, u32[]{:S(2)}, u32[]{:S(2)}) async-start(f32[32,8,128]{2,1,0:T(8,128)} %shard_map.106), calls=%async_computation.4 | async-start | bytes 262144 | tf_op jit(solution)/shard_map/all_to_all | solution.py:323
  73.4 2.2 %shard_map.105 = (f32[512,128]{1,0:T(8,128)S(1)}, f32[512,128]{1,0:T(8,128)S(1)}, bf16[512,128]{1,0:T(8,128)(2,1)}, bf16[512,128]{1,0:T(8,128)(2,1)}) custom-call(bf16[512,128]{1,0:T(8,128)(2,1)S(1)} %copy-done, bf16[512,128]{1,0:T(8,128)(2,1)S(1)} %copy-done.1, f32[512,128]{1,0:T(8,128)S(1)} %get-tuple-element.26.solved_ref, ...), custom_call_target="tpu_custom_call" | custom-call | flops 500000000 | bytes 1179648 | tf_op jit(solution)/shard_map/pallas_call | solution.py:56
  75.5 8.5 %all-to-all-done.4 = f32[32,8,128]{2,1,0:T(8,128)S(1)} async-done(((f32[32,8,128]{2,1,0:T(8,128)}), f32[32,8,128]{2,1,0:T(8,128)S(1)}, u32[]{:S(2)}, u32[]{:S(2)}) %all-to-all-start.4) | async-done | bytes 131104 | tf_op jit(solution)/shard_map/all_to_all | solution.py:323
  84.0 1.1 %shard_map.107 = (bf16[512,128]{1,0:T(8,128)(2,1)}, bf16[512,128]{1,0:T(8,128)(2,1)}, f32[1,128]{1,0:T(1,128)}) custom-call(bf16[512,128]{1,0:T(8,128)(2,1)S(1)} %copy-done, bf16[512,128]{1,0:T(8,128)(2,1)S(1)} %copy-done.1, f32[256,128]{1,0:T(8,128)S(1)} %bitcast.8, f32[512,128]{1,0:T(8,128)S(1)} %get-tuple-element.38.local_k_ref, ...), custom_call_target="tpu_custom_call" | custom-call | flops 100000000 | bytes 917504 | tf_op jit(solution)/shard_map/pallas_call | solution.py:56
  (2 shorter events, 0.0 us)
Async XLA Ops:
  24.2 14.1 %copy-start.2 = (bf16[512,128]{1,0:T(8,128)(2,1)S(1)}, bf16[512,128]{1,0:T(8,128)(2,1)}, u32[]{:S(2)}) copy-start(bf16[512,128]{1,0:T(8,128)(2,1)} %q_ref.1) | copy-start | bytes 393220
  24.2 14.1 %copy-start.3 = (bf16[512,128]{1,0:T(8,128)(2,1)S(1)}, bf16[512,128]{1,0:T(8,128)(2,1)}, u32[]{:S(2)}) copy-start(bf16[512,128]{1,0:T(8,128)(2,1)} %g_ref.3) | copy-start | bytes 393220
  24.2 14.0 %copy-start = (bf16[512,128]{1,0:T(8,128)(2,1)S(1)}, bf16[512,128]{1,0:T(8,128)(2,1)}, u32[]{:S(2)}) copy-start(bf16[512,128]{1,0:T(8,128)(2,1)} %k_ref.7) | copy-start | bytes 393220
  24.2 14.0 %copy-start.1 = (bf16[512,128]{1,0:T(8,128)(2,1)S(1)}, bf16[512,128]{1,0:T(8,128)(2,1)}, u32[]{:S(2)}) copy-start(bf16[512,128]{1,0:T(8,128)(2,1)} %v_ref.7) | copy-start | bytes 393220
  38.2 0.7 copy-start.4
  69.5 14.5 %all-to-all-start.4 = ((f32[32,8,128]{2,1,0:T(8,128)}), f32[32,8,128]{2,1,0:T(8,128)S(1)}, u32[]{:S(2)}, u32[]{:S(2)}) async-start(f32[32,8,128]{2,1,0:T(8,128)} %shard_map.106), calls=%async_computation.4 | async-start | bytes 262144 | tf_op jit(solution)/shard_map/all_to_all | solution.py:323

commit v8 on v7

--- a/solution.py
+++ b/solution.py
@@ -256,7 +256,7 @@
         high, low = split2(lanes(grads[c], adjoint[c]))
         term = mm(turned[c], rows(high, high, low))
         total = term if total is None else total + term
-    part_ref[:D] = total[:, :D].T
+    part_ref[:D] = total[:, :D]
     pairs = total[:, D:] + total[:, D:].T
     part_ref[D : D + 64] = pack(pairs)
     diagonal = jnp.sum(jnp.where(iota2(0) == iota2(1), pairs, 0.0), axis=0, keepdims=True)
@@ -292,7 +292,7 @@
             lanes(ks_high, ks_low, ks_high), rows(a_high, a_high, a_low)
         )
         if suffix is not None:
-            more_k, more_v = finish(k, v, suffix, pairs)
+            more_k, more_v = finish(k, v, suffix, suffix.T, pairs)
             grad_k = grad_k + more_k
             grad_v = grad_v + more_v
         grad_k_ref[at] = grad_k
@@ -305,15 +305,16 @@
             pairs = pair if pairs is None else pairs + pair
 
 
-def finish(k, v, suffix, pairs):
-    t_high, t_low = split2(suffix.T)
+def finish(k, v, suffix, turned, pairs):
+    t_high, t_low = split2(turned)
     weights = rows(*split2(suffix), *split2(-pairs))
     return mm(lanes(v, v, k, k), weights), mm(lanes(k, k), rows(t_high, t_low))
 
 
 def last_kernel(k_ref, v_ref, state_ref, local_k_ref, local_v_ref, grad_k_ref, grad_v_ref, gain_ref):
     pairs = unpack(state_ref[D : D + 64], state_ref[D + 64 : D + 65])
-    grad_k, grad_v = finish(k_ref[...], v_ref[...], state_ref[:D], pairs)
+    turned = state_ref[:D]
+    grad_k, grad_v = finish(k_ref[...], v_ref[...], turned.T, turned, pairs)
     grad_v_ref[...] = (local_v_ref[...] + grad_v).astype(BF16)
     grad_k_ref[...] = (local_k_ref[...] + grad_k).astype(BF16)
     gain_ref[...] = jnp.sum(state_ref[D + 72 : D + 80], axis=0, keepdims=True)

time: 85.5 us -> 85.5 us (level)
  no operation moved by 1% of the time
where the time goes in v8:
time: 85.5 us; the launch traced here: 85.1 us
  blocking collectives  58.4 us (68%)
  Pallas kernels  12.4 us (15%)
  waiting for transfers between devices  8.46 us (10%)
  starting transfers between devices  3.86 us (5%)
  between operations  1.34 us (2%)
    all_to_all x4, blocking collectives, exchange(): return lax.all_to_all(array, axis, split_axis=0, concat_axis=0, tiled=True)  58.4 us
    pallas_call x7, Pallas kernels, call(): pl.pallas_call(kernel, out_shape=[jax.ShapeDtypeStruct(s, t) for s, t in...  12.4 us
    all_to_all x1, waiting for transfers between devices, exchange(): return lax.all_to_all(array, axis, split_axis=0, concat_axis=0, tiled=True)  8.46 us
    all_to_all x1, starting transfers between devices, exchange(): return lax.all_to_all(array, axis, split_axis=0, concat_axis=0, tiled=True)  3.86 us
  transfers between devices with their start and end apart: 1, of which 1 were waited for; matrix products, arithmetic and copies ran while one was open for 0% of the time, Pallas kernels for 3%

profile of v8, /device:TPU:8, one launch (start us, length us, event | category | flops | bytes accessed | tf_op | source)
XLA Modules:
  0.0 85.1 jit_solution(3827414320064441074)
XLA Ops:
  1.3 1.2 %shard_map.101 = f32[256,128]{1,0:T(8,128)S(1)} custom-call(bf16[512,128]{1,0:T(8,128)(2,1)} %k_ref.7, bf16[512,128]{1,0:T(8,128)(2,1)} %v_ref.7), custom_call_target="tpu_custom_call" | custom-call | flops 33554432 | bytes 262144 | tf_op jit(solution)/shard_map/pallas_call | solution.py:56
  2.5 21.6 %all_to_all.25.a_ref = f32[32,8,128]{2,1,0:T(8,128)S(1)} all-to-all(f32[32,8,128]{2,1,0:T(8,128)S(1)} %bitcast.9), channel_id=1, replica_groups=mesh['z'=8,'x'=4,'y'=4,'core'=2] {'z','x'}, dimensions={0} | all-to-all | bytes 262144 | tf_op jit(solution)/shard_map/all_to_all | solution.py:324
  24.2 0.0 copy-start.2
  24.2 0.0 copy-start.3
  24.2 0.0 copy-start
  24.2 0.0 copy-start.1
  24.2 14.0 %all_to_all.26 = f32[32,8,128]{2,1,0:T(8,128)S(1)} all-to-all(f32[32,8,128]{2,1,0:T(8,128)S(1)} %shard_map.102), channel_id=1, replica_groups=mesh['z'=8,'x'=4,'y'=4,'core'=2] {'z','x'}, dimensions={0} | all-to-all | bytes 262144 | tf_op jit(solution)/shard_map/all_to_all | solution.py:324
  38.2 0.0 copy-start.4
  38.2 0.0 copy-done.2
  38.2 0.0 copy-done.3
  38.2 0.0 copy-done
  38.2 0.0 copy-done.1
  38.2 0.6 copy-done.4
  38.9 3.5 %shard_map.103 = (f32[512,128]{1,0:T(8,128)S(1)}, f32[512,128]{1,0:T(8,128)S(1)}, f32[8,8,128]{2,1,0:T(8,128)S(1)}, bf16[4,256,256]{2,1,0:T(8,128)(2,1)S(1)}, bf...) custom-call(f32[1,128]{1,0:T(1,128)S(1)} %broadcast_in_dim.8.ridge_ref, f32[1,128]{1,0:T(1,128)S(1)} %bitcast.12, ...), custom_call_target="tpu_custom_call" | custom-call | flops 1000000000 | bytes 656384 | tf_op jit(solution)/shard_map/pallas_call | solution.py:56
  42.3 8.7 %all_to_all.27.sums_ref = f32[8,8,128]{2,1,0:T(8,128)S(1)} all-to-all(f32[8,8,128]{2,1,0:T(8,128)S(1)} %get-tuple-element.27), channel_id=1, replica_groups=mesh['z'=8,'x'=4,'y'=4,'core'=2] {'core','y'}, dimensions={0} | all-to-all | bytes 65536 | tf_op jit(solution)/shard_map/all_to_all | solution.py:324
  51.0 3.7 %shard_map.104 = (bf16[512,128]{1,0:T(8,128)(2,1)S(1)}, f32[512,128]{1,0:T(8,128)S(1)}, f32[512,128]{1,0:T(8,128)S(1)}, f32[256,128]{1,0:T(8,128)S(1)}) custom-call(f32[1,128]{1,0:T(1,128)S(1)} %bitcast.13, bf16[512,128]{1,0:T(8,128)(2,1)S(1)} %copy-done, bf16[512,128]{1,0:T(8,128)(2,1)S(1)} %copy-done.1, bf16[512,128]{1,0:T(8,128)(2,1)S(1)} %copy-done.3, ...), custom_call_target="tpu_custom_call" | custom-call | flops 1000000000 | bytes 2130432 | tf_op jit(solution)/shard_map/pallas_call | solution.py:56
  54.7 14.1 %all_to_all.28.a_ref = f32[32,8,128]{2,1,0:T(8,128)S(1)} all-to-all(f32[32,8,128]{2,1,0:T(8,128)S(1)} %bitcast.10), channel_id=1, replica_groups=mesh['z'=8,'x'=4,'y'=4,'core'=2] {'z','x'}, dimensions={0} | all-to-all | bytes 262144 | tf_op jit(solution)/shard_map/all_to_all | solution.py:324
  68.8 0.7 shard_map.106
  69.5 3.9 %all-to-all-start.4 = ((f32[32,8,128]{2,1,0:T(8,128)}), f32[32,8,128]{2,1,0:T(8,128)S(1)}, u32[]{:S(2)}, u32[]{:S(2)}) async-start(f32[32,8,128]{2,1,0:T(8,128)} %shard_map.106), calls=%async_computation.4 | async-start | bytes 262144 | tf_op jit(solution)/shard_map/all_to_all | solution.py:324
  73.3 2.2 %shard_map.105 = (f32[512,128]{1,0:T(8,128)S(1)}, f32[512,128]{1,0:T(8,128)S(1)}, bf16[512,128]{1,0:T(8,128)(2,1)}, bf16[512,128]{1,0:T(8,128)(2,1)}) custom-call(bf16[512,128]{1,0:T(8,128)(2,1)S(1)} %copy-done, bf16[512,128]{1,0:T(8,128)(2,1)S(1)} %copy-done.1, f32[512,128]{1,0:T(8,128)S(1)} %get-tuple-element.26.solved_ref, ...), custom_call_target="tpu_custom_call" | custom-call | flops 500000000 | bytes 1179648 | tf_op jit(solution)/shard_map/pallas_call | solution.py:56
  75.5 8.5 %all-to-all-done.4 = f32[32,8,128]{2,1,0:T(8,128)S(1)} async-done(((f32[32,8,128]{2,1,0:T(8,128)}), f32[32,8,128]{2,1,0:T(8,128)S(1)}, u32[]{:S(2)}, u32[]{:S(2)}) %all-to-all-start.4) | async-done | bytes 131104 | tf_op jit(solution)/shard_map/all_to_all | solution.py:324
  83.9 1.2 %shard_map.107 = (bf16[512,128]{1,0:T(8,128)(2,1)}, bf16[512,128]{1,0:T(8,128)(2,1)}, f32[1,128]{1,0:T(1,128)}) custom-call(bf16[512,128]{1,0:T(8,128)(2,1)S(1)} %copy-done, bf16[512,128]{1,0:T(8,128)(2,1)S(1)} %copy-done.1, f32[256,128]{1,0:T(8,128)S(1)} %bitcast.8, f32[512,128]{1,0:T(8,128)S(1)} %get-tuple-element.38.local_k_ref, ...), custom_call_target="tpu_custom_call" | custom-call | flops 100000000 | bytes 917504 | tf_op jit(solution)/shard_map/pallas_call | solution.py:56
  (2 shorter events, 0.0 us)
Async XLA Ops:
  24.2 14.1 %copy-start.2 = (bf16[512,128]{1,0:T(8,128)(2,1)S(1)}, bf16[512,128]{1,0:T(8,128)(2,1)}, u32[]{:S(2)}) copy-start(bf16[512,128]{1,0:T(8,128)(2,1)} %q_ref.1) | copy-start | bytes 393220
  24.2 14.1 %copy-start.3 = (bf16[512,128]{1,0:T(8,128)(2,1)S(1)}, bf16[512,128]{1,0:T(8,128)(2,1)}, u32[]{:S(2)}) copy-start(bf16[512,128]{1,0:T(8,128)(2,1)} %g_ref.3) | copy-start | bytes 393220
  24.2 14.0 %copy-start = (bf16[512,128]{1,0:T(8,128)(2,1)S(1)}, bf16[512,128]{1,0:T(8,128)(2,1)}, u32[]{:S(2)}) copy-start(bf16[512,128]{1,0:T(8,128)(2,1)} %k_ref.7) | copy-start | bytes 393220
  24.2 14.0 %copy-start.1 = (bf16[512,128]{1,0:T(8,128)(2,1)S(1)}, bf16[512,128]{1,0:T(8,128)(2,1)}, u32[]{:S(2)}) copy-start(bf16[512,128]{1,0:T(8,128)(2,1)} %v_ref.7) | copy-start | bytes 393220
  38.2 0.7 copy-start.4
  69.5 14.5 %all-to-all-start.4 = ((f32[32,8,128]{2,1,0:T(8,128)}), f32[32,8,128]{2,1,0:T(8,128)S(1)}, u32[]{:S(2)}, u32[]{:S(2)}) async-start(f32[32,8,128]{2,1,0:T(8,128)} %shard_map.106), calls=%async_computation.4 | async-start | bytes 262144 | tf_op jit(solution)/shard_map/all_to_all | solution.py:324
